TPU v7x, 128 devices: a whole 4x4x4 slice. The times are simulated.
128 devices in a mesh: gx: 8 (over x, core), gy: 16 (over y, z).
Axes of the slice: x: 4, y: 4, z: 4, core: 2. Of those that a mesh axis runs over, the one named last changes fastest.
Arguments:
- residual: float32 [2, 2097152], P(None, ('gx', 'gy')), may hold values from -15 to 15
- cam_jacobian: float32 [2, 9, 2097152], P(None, None, ('gx', 'gy')), may hold values from -0.3 to 0.3
- point_jacobian: float32 [2, 3, 2097152], P(None, None, ('gx', 'gy')), may hold values from -1.5 to 1.5
- obs_camera: int32 [2097152], P(('gx', 'gy')), may hold values from 0 to 16383
- obs_slot: int32 [2097152], P(('gx', 'gy')), may hold values from 0 to 127, as said below
- tile_offset: int32 [4096], P(('gx', 'gy')), may hold values from 0 to 1920, as said below
- damping: float32 [262144], P(('gx', 'gy')), may hold values from 0.3 to 3
- camera_slot: int32 [16384], replicated, may hold values from 0 to 16383, as said below
Outputs:
- reduced: float32 [9, 16384], P(None, ('gx', 'gy'))
- cost: float32 [], replicated
- grad_norm: float32 [], replicated
Inputs may be any that keep to these rules, and one draw needn't show every extreme that they name: `obs_slot`: on each device observations are ordered by point; every observation's point lies in its tile's window of 128 points starting at tile_offset. `tile_offset`: windows lie within the device's 2048 points and do not fall from tile to tile. `camera_slot`: each position of the owners' layout is taken by exactly one camera.
All inputs are finite; a program needn't handle non-finite values.
Results may differ from a plain program's by a relative error of at most 0.000096.
Values sent between devices are 32-bit elements; how exact they have to be, the bound alone decides.
A program may use at most 64 MiB of HBM per device.

v0:
```python
import functools

import jax
import jax.numpy as jnp
from jax import lax
from jax.sharding import Mesh
from jax.sharding import PartitionSpec as P

GX_GY = ("gx_0", "gx_1", "gy_0", "gy_1")


def reduced_to_own(tiles, axes, order):
    inside = tiles.shape[1:]
    tiles = tiles.reshape(*(lax.axis_size(a) for a in axes), *inside)
    tiles = jnp.moveaxis(tiles, order, range(len(axes))).reshape(-1, *inside)
    for k in order:
        tiles = lax.psum_scatter(tiles, axes[k], scatter_dimension=0, tiled=True)
    return tiles[0]


def cut_along(array, dim, devices):
    shape = array.shape
    tiles = array.reshape(*shape[:dim], devices, shape[dim] // devices, *shape[dim + 1 :])
    return jnp.moveaxis(tiles, dim, 0)


def sum_by_axis(array, axes, order, dim):
    devices = lax.axis_size(axes)
    return reduced_to_own(cut_along(array, dim, devices), axes, order)


def one_axis_at_a_time(array, axes):
    return functools.reduce(lax.psum, axes, array)


def block_solve(entries, rhs):
    comp_aa = entries[0]
    comp_ab = entries[1]
    comp_ac = entries[2]
    comp_bb = entries[3]
    comp_bc = entries[4]
    comp_cc = entries[5]
    cof_aa = comp_bb * comp_cc - comp_bc * comp_bc
    cof_ab = comp_ac * comp_bc - comp_ab * comp_cc
    cof_ac = comp_ab * comp_bc - comp_ac * comp_bb
    cof_bb = comp_aa * comp_cc - comp_ac * comp_ac
    cof_bc = comp_ab * comp_ac - comp_aa * comp_bc
    cof_cc = comp_aa * comp_bb - comp_ab * comp_ab
    determ = comp_aa * cof_aa + comp_ab * cof_ab + comp_ac * cof_ac
    first = (cof_aa * rhs[0] + cof_ab * rhs[1] + cof_ac * rhs[2]) / determ
    second = (cof_ab * rhs[0] + cof_bb * rhs[1] + cof_bc * rhs[2]) / determ
    third = (cof_ac * rhs[0] + cof_bc * rhs[1] + cof_cc * rhs[2]) / determ
    return jnp.stack([first, second, third])


def point_features(residual, point_jacobian):
    grad_obs = jnp.sum(point_jacobian * residual[:, None, :], axis=0)
    pairs = [(0, 0), (0, 1), (0, 2), (1, 1), (1, 2), (2, 2)]
    products = [
        jnp.sum(point_jacobian[:, left] * point_jacobian[:, right], axis=0) for left, right in pairs
    ]
    return jnp.concatenate([grad_obs, jnp.stack(products)], axis=0)


def block_length(n_obs):
    return min(n_obs, max(512, n_obs // 16))


def onehot_sums(values, index, count):
    rows, n_obs = values.shape
    length = block_length(n_obs)
    blocks = n_obs // length
    value_blocks = jnp.moveaxis(values.reshape(rows, blocks, length), 1, 0)
    index_blocks = index.reshape(blocks, length)
    columns = jnp.arange(count, dtype=jnp.int32)

    def add_block(total, pair):
        block_values, block_index = pair
        onehot = (block_index[:, None] == columns[None, :]).astype(jnp.float32)
        return (total + jnp.dot(block_values, onehot, precision=lax.Precision.HIGHEST), None)

    start = jnp.zeros((rows, count), jnp.float32)
    total, _ = lax.scan(add_block, start, (value_blocks, index_blocks))
    return total


def onehot_take(table, index):
    rows, count = table.shape
    n_obs = index.shape[0]
    length = block_length(n_obs)
    blocks = n_obs // length
    index_blocks = index.reshape(blocks, length)
    columns = jnp.arange(count, dtype=jnp.int32)

    def take_block(block_index):
        onehot = (columns[:, None] == block_index[None, :]).astype(jnp.float32)
        return jnp.dot(table, onehot, precision=lax.Precision.HIGHEST)

    taken = lax.map(take_block, index_blocks)
    return jnp.moveaxis(taken, 0, 1).reshape(rows, n_obs)


def on_device(
    residual, cam_jacobian, point_jacobian, obs_camera, obs_slot, tile_offset, damping, camera_slot
):
    n_obs = residual.shape[1]
    n_tiles = tile_offset.shape[0]
    tile_len = n_obs // n_tiles
    point_count = damping.shape[0]
    camera_count = camera_slot.shape[0]
    devices = lax.axis_size(GX_GY)
    cam_slots = camera_slot[obs_camera]
    grad_obs = jnp.sum(cam_jacobian * residual[:, None, :], axis=0)
    cost_part = jnp.sum(residual * residual)
    features = point_features(residual, point_jacobian)
    slot_tiles = obs_slot.reshape(n_tiles, tile_len)
    point_index = (tile_offset[:, None] + slot_tiles).reshape(-1)
    point_sums = onehot_sums(features, point_index, point_count)
    point_grad = point_sums[:3]
    diag_mask = jnp.array([1.0, 0.0, 0.0, 1.0, 0.0, 1.0], jnp.float32)[:, None]
    entries = point_sums[3:] + diag_mask * damping[None, :]
    step_point = block_solve(entries, point_grad)
    step_obs = onehot_take(step_point, point_index)
    moved = jnp.sum(point_jacobian * step_obs[None, :, :], axis=1)
    coupling_obs = jnp.sum(cam_jacobian * moved[:, None, :], axis=0)
    point_square = jnp.sum(point_grad * point_grad)
    both_obs = jnp.concatenate([grad_obs, coupling_obs], axis=0)
    both_buffer = onehot_sums(both_obs, cam_slots, camera_count)
    both_share = sum_by_axis(both_buffer, GX_GY, (1, 0, 2, 3), 1)
    grad_share = both_share[:9]
    coupling_share = both_share[9:]
    reduced = coupling_share - grad_share
    camera_square = jnp.sum(grad_share * grad_share)
    cost_total, point_total, camera_sum = (
        one_axis_at_a_time(cost_part, GX_GY),
        one_axis_at_a_time(point_square, GX_GY),
        one_axis_at_a_time(camera_square, GX_GY),
    )
    cost = cost_total / (2.0 * n_obs * devices)
    grad_norm = jnp.sqrt(
        (camera_sum + point_total) / (9.0 * camera_count + 3.0 * point_count * devices) + 1e-06
    )
    return (reduced, cost, grad_norm)


def solution(mesh):
    finer = Mesh(mesh.devices.reshape(4, 2, 4, 4), ("gx_0", "gx_1", "gy_0", "gy_1"))
    in_specs = (
        P(None, GX_GY),
        P(None, None, GX_GY),
        P(None, None, GX_GY),
        P(GX_GY),
        P(GX_GY),
        P(GX_GY),
        P(GX_GY),
        P(),
    )
    out_specs = (P(None, GX_GY), P(), P())
    return jax.shard_map(
        on_device, mesh=finer, in_specs=in_specs, out_specs=out_specs, check_vma=False
    )
```

profile of v0, /device:TPU:1, one launch (start us, length us, event | category | flops | bytes accessed | tf_op | source)
XLA Modules:
  0.0 717.7 jit_solution(4714866338831503618)
XLA Ops:
  12.0 44.6 %while.34 = (s32[]{:T(128)}, f32[9,2048]{1,0:T(8,128)S(1)}, f32[16,9,1024]{2,1,0:T(8,128)S(1)}, s32[16,1024]{1,0:T(8,128)S(1)}, s32[]{:T(128)}, /*index=5*/s32[]{:T(128)}) while((s32[]{:T(128)}, f32[9,2048]{1,0:T(8,128)S(1)}, f32[16,9,1024]{2,1,0:T(8,128)S(1)}, s32[16,1024]{1,0:T(8,128)S(1)}, s32[]{:T(128)}, ...), condition=%wide.region_9.10_spmd.clone, body=%wide.region_8.0_spmd.clone.sunk | while | flops 228626432 | bytes 282711 | solution.py:83
  57.6 64.2 %while.33 = (s32[]{:T(128)}, f32[16,3,1024]{2,1,0:T(4,128)}, s32[16,1024]{1,0:T(8,128)S(1)}, f32[3,2048]{1,0:T(4,128)}, s32[]{:T(128)}) while((s32[]{:T(128)}, f32[16,3,1024]{2,1,0:T(4,128)}, s32[16,1024]{1,0:T(8,128)S(1)}, f32[3,2048]{1,0:T(4,128)}, s32[]{:T(128)}) %tuple.89), condition=%wide.region_11.12_spmd.clone, body=%wide.region_10.11_spmd.clone.sunk | while | flops 77594624 | bytes 62017 | solution.py:99
  128.0 90.5 %gather_fusion = s32[16384]{0:T(1024)S(1)} fusion(s32[16384]{0:T(1024)S(1)} %copy-done, s32[16384]{0:T(1024)S(1)} %fusion.19), kind=kCustom, calls=%fused_computation | custom fusion | bytes 196608 | tf_op jit(solution)/shard_map/gather | solution.py:112
  218.5 352.9 %while.35 = (s32[]{:T(128)}, f32[18,16384]{1,0:T(8,128)S(1)}, f32[16,18,1024]{2,0,1:T(8,128)S(1)}, s32[16,1024]{1,0:T(8,128)S(1)}, s32[]{:T(128)}, /*index=5*/s32[]{:T(128)}) while((s32[]{:T(128)}, f32[18,16384]{1,0:T(8,128)S(1)}, f32[16,18,1024]{2,0,1:T(8,128)S(1)}, s32[16,1024]{1,0:T(8,128)S(1)}, s32[]{:T(128)}, ...), condition=%wide.region_15.16_spmd.clone, body=%wide.region_14.15_spmd.clone.sunk | while | flops 3641245696 | bytes 2592855 | solution.py:83
  218.8 21.9 %fusion.30 = f32[18,16384]{1,0:T(8,128)S(1)} fusion(s32[1024]{0:T(1024)S(1)} %bitcast.79, f32[18,16384]{1,0:T(8,128)S(1)} %get-tuple-element.306, pred[]{:T(512)S(6)} %compare.7, f32[1,18,1024]{2,0,1:T(1,128)S(1)} %constant_dynamic-slice_fusion.12), kind=kOutput, calls=%fused_computation.21.clone.1 | convolution fusion | flops 3641245696 | bytes 2437121 | tf_op jit(solution)/shard_map/while/body/eval_jaxpr/dot_general | solution.py:80
  240.9 21.9 %fusion.30 = f32[18,16384]{1,0:T(8,128)S(1)} fusion(s32[1024]{0:T(1024)S(1)} %bitcast.79, f32[18,16384]{1,0:T(8,128)S(1)} %get-tuple-element.306, pred[]{:T(512)S(6)} %compare.7, f32[1,18,1024]{2,0,1:T(1,128)S(1)} %constant_dynamic-slice_fusion.12), kind=kOutput, calls=%fused_computation.21.clone.1 | convolution fusion | flops 3641245696 | bytes 2437121 | tf_op jit(solution)/shard_map/while/body/eval_jaxpr/dot_general | solution.py:80
  262.9 21.9 %fusion.30 = f32[18,16384]{1,0:T(8,128)S(1)} fusion(s32[1024]{0:T(1024)S(1)} %bitcast.79, f32[18,16384]{1,0:T(8,128)S(1)} %get-tuple-element.306, pred[]{:T(512)S(6)} %compare.7, f32[1,18,1024]{2,0,1:T(1,128)S(1)} %constant_dynamic-slice_fusion.12), kind=kOutput, calls=%fused_computation.21.clone.1 | convolution fusion | flops 3641245696 | bytes 2437121 | tf_op jit(solution)/shard_map/while/body/eval_jaxpr/dot_general | solution.py:80
  285.0 21.9 %fusion.30 = f32[18,16384]{1,0:T(8,128)S(1)} fusion(s32[1024]{0:T(1024)S(1)} %bitcast.79, f32[18,16384]{1,0:T(8,128)S(1)} %get-tuple-element.306, pred[]{:T(512)S(6)} %compare.7, f32[1,18,1024]{2,0,1:T(1,128)S(1)} %constant_dynamic-slice_fusion.12), kind=kOutput, calls=%fused_computation.21.clone.1 | convolution fusion | flops 3641245696 | bytes 2437121 | tf_op jit(solution)/shard_map/while/body/eval_jaxpr/dot_general | solution.py:80
  307.0 21.9 %fusion.30 = f32[18,16384]{1,0:T(8,128)S(1)} fusion(s32[1024]{0:T(1024)S(1)} %bitcast.79, f32[18,16384]{1,0:T(8,128)S(1)} %get-tuple-element.306, pred[]{:T(512)S(6)} %compare.7, f32[1,18,1024]{2,0,1:T(1,128)S(1)} %constant_dynamic-slice_fusion.12), kind=kOutput, calls=%fused_computation.21.clone.1 | convolution fusion | flops 3641245696 | bytes 2437121 | tf_op jit(solution)/shard_map/while/body/eval_jaxpr/dot_general | solution.py:80
  329.0 21.9 %fusion.30 = f32[18,16384]{1,0:T(8,128)S(1)} fusion(s32[1024]{0:T(1024)S(1)} %bitcast.79, f32[18,16384]{1,0:T(8,128)S(1)} %get-tuple-element.306, pred[]{:T(512)S(6)} %compare.7, f32[1,18,1024]{2,0,1:T(1,128)S(1)} %constant_dynamic-slice_fusion.12), kind=kOutput, calls=%fused_computation.21.clone.1 | convolution fusion | flops 3641245696 | bytes 2437121 | tf_op jit(solution)/shard_map/while/body/eval_jaxpr/dot_general | solution.py:80
  351.1 21.9 %fusion.30 = f32[18,16384]{1,0:T(8,128)S(1)} fusion(s32[1024]{0:T(1024)S(1)} %bitcast.79, f32[18,16384]{1,0:T(8,128)S(1)} %get-tuple-element.306, pred[]{:T(512)S(6)} %compare.7, f32[1,18,1024]{2,0,1:T(1,128)S(1)} %constant_dynamic-slice_fusion.12), kind=kOutput, calls=%fused_computation.21.clone.1 | convolution fusion | flops 3641245696 | bytes 2437121 | tf_op jit(solution)/shard_map/while/body/eval_jaxpr/dot_general | solution.py:80
  373.1 21.9 %fusion.30 = f32[18,16384]{1,0:T(8,128)S(1)} fusion(s32[1024]{0:T(1024)S(1)} %bitcast.79, f32[18,16384]{1,0:T(8,128)S(1)} %get-tuple-element.306, pred[]{:T(512)S(6)} %compare.7, f32[1,18,1024]{2,0,1:T(1,128)S(1)} %constant_dynamic-slice_fusion.12), kind=kOutput, calls=%fused_computation.21.clone.1 | convolution fusion | flops 3641245696 | bytes 2437121 | tf_op jit(solution)/shard_map/while/body/eval_jaxpr/dot_general | solution.py:80
  395.2 21.9 %fusion.30 = f32[18,16384]{1,0:T(8,128)S(1)} fusion(s32[1024]{0:T(1024)S(1)} %bitcast.79, f32[18,16384]{1,0:T(8,128)S(1)} %get-tuple-element.306, pred[]{:T(512)S(6)} %compare.7, f32[1,18,1024]{2,0,1:T(1,128)S(1)} %constant_dynamic-slice_fusion.12), kind=kOutput, calls=%fused_computation.21.clone.1 | convolution fusion | flops 3641245696 | bytes 2437121 | tf_op jit(solution)/shard_map/while/body/eval_jaxpr/dot_general | solution.py:80
  417.2 21.9 %fusion.30 = f32[18,16384]{1,0:T(8,128)S(1)} fusion(s32[1024]{0:T(1024)S(1)} %bitcast.79, f32[18,16384]{1,0:T(8,128)S(1)} %get-tuple-element.306, pred[]{:T(512)S(6)} %compare.7, f32[1,18,1024]{2,0,1:T(1,128)S(1)} %constant_dynamic-slice_fusion.12), kind=kOutput, calls=%fused_computation.21.clone.1 | convolution fusion | flops 3641245696 | bytes 2437121 | tf_op jit(solution)/shard_map/while/body/eval_jaxpr/dot_general | solution.py:80
  439.2 21.9 %fusion.30 = f32[18,16384]{1,0:T(8,128)S(1)} fusion(s32[1024]{0:T(1024)S(1)} %bitcast.79, f32[18,16384]{1,0:T(8,128)S(1)} %get-tuple-element.306, pred[]{:T(512)S(6)} %compare.7, f32[1,18,1024]{2,0,1:T(1,128)S(1)} %constant_dynamic-slice_fusion.12), kind=kOutput, calls=%fused_computation.21.clone.1 | convolution fusion | flops 3641245696 | bytes 2437121 | tf_op jit(solution)/shard_map/while/body/eval_jaxpr/dot_general | solution.py:80
  461.3 21.9 %fusion.30 = f32[18,16384]{1,0:T(8,128)S(1)} fusion(s32[1024]{0:T(1024)S(1)} %bitcast.79, f32[18,16384]{1,0:T(8,128)S(1)} %get-tuple-element.306, pred[]{:T(512)S(6)} %compare.7, f32[1,18,1024]{2,0,1:T(1,128)S(1)} %constant_dynamic-slice_fusion.12), kind=kOutput, calls=%fused_computation.21.clone.1 | convolution fusion | flops 3641245696 | bytes 2437121 | tf_op jit(solution)/shard_map/while/body/eval_jaxpr/dot_general | solution.py:80
  483.3 21.9 %fusion.30 = f32[18,16384]{1,0:T(8,128)S(1)} fusion(s32[1024]{0:T(1024)S(1)} %bitcast.79, f32[18,16384]{1,0:T(8,128)S(1)} %get-tuple-element.306, pred[]{:T(512)S(6)} %compare.7, f32[1,18,1024]{2,0,1:T(1,128)S(1)} %constant_dynamic-slice_fusion.12), kind=kOutput, calls=%fused_computation.21.clone.1 | convolution fusion | flops 3641245696 | bytes 2437121 | tf_op jit(solution)/shard_map/while/body/eval_jaxpr/dot_general | solution.py:80
  505.4 21.9 %fusion.30 = f32[18,16384]{1,0:T(8,128)S(1)} fusion(s32[1024]{0:T(1024)S(1)} %bitcast.79, f32[18,16384]{1,0:T(8,128)S(1)} %get-tuple-element.306, pred[]{:T(512)S(6)} %compare.7, f32[1,18,1024]{2,0,1:T(1,128)S(1)} %constant_dynamic-slice_fusion.12), kind=kOutput, calls=%fused_computation.21.clone.1 | convolution fusion | flops 3641245696 | bytes 2437121 | tf_op jit(solution)/shard_map/while/body/eval_jaxpr/dot_general | solution.py:80
  527.4 21.9 %fusion.30 = f32[18,16384]{1,0:T(8,128)S(1)} fusion(s32[1024]{0:T(1024)S(1)} %bitcast.79, f32[18,16384]{1,0:T(8,128)S(1)} %get-tuple-element.306, pred[]{:T(512)S(6)} %compare.7, f32[1,18,1024]{2,0,1:T(1,128)S(1)} %constant_dynamic-slice_fusion.12), kind=kOutput, calls=%fused_computation.21.clone.1 | convolution fusion | flops 3641245696 | bytes 2437121 | tf_op jit(solution)/shard_map/while/body/eval_jaxpr/dot_general | solution.py:80
  549.5 21.9 %fusion.30 = f32[18,16384]{1,0:T(8,128)S(1)} fusion(s32[1024]{0:T(1024)S(1)} %bitcast.79, f32[18,16384]{1,0:T(8,128)S(1)} %get-tuple-element.306, pred[]{:T(512)S(6)} %compare.7, f32[1,18,1024]{2,0,1:T(1,128)S(1)} %constant_dynamic-slice_fusion.12), kind=kOutput, calls=%fused_computation.21.clone.1 | convolution fusion | flops 3641245696 | bytes 2437121 | tf_op jit(solution)/shard_map/while/body/eval_jaxpr/dot_general | solution.py:80
  573.2 14.9 %reduce-scatter.5.cloned.1.call-done = f32[64,18,128]{2,0,1:T(8,128)} async-done(((f32[128,18,128]{2,0,1:T(8,128)}), f32[64,18,128]{2,0,1:T(8,128)}) %reduce-scatter.5.cloned.1.call-update) | async-done | bytes 589840 | tf_op jit(solution)/shard_map/reduce_scatter | solution.py:17
  588.2 23.2 %reduce-scatter.7.cloned.1.call-done = f32[16,18,128]{2,0,1:T(8,128)} async-done(((f32[64,18,128]{2,0,1:T(8,128)}), f32[16,18,128]{2,0,1:T(8,128)}) %reduce-scatter.7.cloned.1.call-update) | async-done | bytes 147472 | tf_op jit(solution)/shard_map/reduce_scatter | solution.py:17
  614.6 40.3 %all-reduce.8.cloned.1.call-done = f32[16,18,128]{2,0,1:T(8,128)} async-done(((f32[16,18,128]{2,0,1:T(8,128)}), f32[16,18,128]{2,0,1:T(8,128)}) %all-reduce.8.cloned.1.call-update) | async-done | bytes 147472
  655.8 13.9 %all-reduce.1 = f32[4,18,128]{2,0,1:T(4,128)S(1)} all-reduce(f32[4,18,128]{2,0,1:T(4,128)S(1)} %constant_dynamic-slice_fusion.4), channel_id=5, replica_groups=mesh['gx_0'=4,'gx_1'=2,'gy_0'=4,'gy_1'=4] {'gy_1'}, use_global_device_ids=true, to_apply=%region_19.20.clone | all-reduce | flops 9216 | bytes 73728
  (160 shorter events, 163.3 us)
Async XLA Ops:
  7.2 120.8 %copy-start = (s32[16384]{0:T(1024)S(1)}, s32[16384]{0:T(1024)}, u32[]{:S(2)}) copy-start(s32[16384]{0:T(1024)} %param.22) | copy-start | bytes 196612
  7.2 3.8 copy-start.8
  7.2 4.0 copy-start.4
  7.2 580.9 %reduce-scatter.5.cloned.1.call-start = ((), (), s32[]{:S(2)}) async-start(), calls=%async_computation.2 | async-start | bytes 1769472 | tf_op jit(solution)/shard_map/reduce_scatter | solution.py:17
  12.0 44.7 %copy-start.6 = (f32[2048]{0:T(1024)S(1)}, f32[2048]{0:T(1024)}, u32[]{:S(2)}) copy-start(f32[2048]{0:T(1024)} %param.21) | copy-start | bytes 24580
  12.0 44.7 %copy-start.7 = (f32[6]{0:T(128)S(1)}, f32[6]{0:T(128)}, u32[]{:S(2)}) copy-start(f32[6]{0:T(128)} %constant.45.clone) | copy-start | bytes 76
  57.6 64.2 %copy-start.1 = (f32[2,3,16384]{2,0,1:T(2,128)S(1)}, f32[2,3,16384]{2,0,1:T(2,128)}, u32[]{:S(2)}) copy-start(f32[2,3,16384]{2,0,1:T(2,128)} %param.17) | copy-start | bytes 1179652
  57.6 65.4 %copy-start.2 = (f32[2,16384]{1,0:T(2,128)S(1)}, f32[2,16384]{1,0:T(2,128)}, u32[]{:S(2)}) copy-start(f32[2,16384]{1,0:T(2,128)} %param.15) | copy-start | bytes 393220
  57.6 65.5 %copy-start.3 = (f32[2,9,16384]{2,0,1:T(2,128)S(1)}, f32[2,9,16384]{2,0,1:T(2,128)}, u32[]{:S(2)}) copy-start(f32[2,9,16384]{2,0,1:T(2,128)} %param.16) | copy-start | bytes 3538948
  127.1 0.8 copy-start.5
  573.1 38.9 %copy-start.10 = (u32[128]{0:T(128)S(1)}, u32[128]{0:T(128)}, u32[]{:S(2)}) copy-start(u32[128]{0:T(128)} %constant.49) | copy-start | bytes 1540
  573.1 39.5 %copy-start.9 = (u32[128]{0:T(128)S(1)}, u32[128]{0:T(128)}, u32[]{:S(2)}) copy-start(u32[128]{0:T(128)} %constant.53) | copy-start | bytes 1540
  573.1 38.3 %reduce-scatter.7.cloned.1.call-start = ((), (), s32[]{:S(2)}) async-start(), calls=%async_computation.3 | async-start | bytes 737280 | tf_op jit(solution)/shard_map/reduce_scatter | solution.py:17
  588.1 66.8 %all-reduce.8.cloned.1.call-start = ((), (), s32[]{:S(2)}) async-start(), calls=%async_computation.4 | async-start | bytes 294912
Sparse Core Ops, SparseCore 0:
  573.2 14.8 reduce-scatter.4
  590.5 20.8 reduce-scatter.6
  613.7 41.1 all-reduce.7
where the time goes:
time: 722 us; the launch traced here: 718 us
  matrix products  459 us (64%)
  local copies, waits for them, and re-layouts  99.1 us (14%)
  waiting for transfers between devices  78.5 us (11%)
  blocking collectives  48.6 us (7%)
  between operations  19.5 us (3%)
  other arithmetic  11.5 us (2%)
    dot_general x32, matrix products, add_block(): jnp.dot(block_values, onehot, precision=lax.Precision.HIGHEST)  395 us
    gather x1, local copies, waits for them, and re-layouts, on_device(): cam_slots = camera_slot[obs_camera]  90.5 us
    dot_general x16, matrix products, take_block(): return jnp.dot(table, onehot, precision=lax.Precision.HIGHEST)  64 us
    unnamed x4, waiting for transfers between devices  40.4 us
    reduce_scatter x2, waiting for transfers between devices, reduced_to_own(): tiles = lax.psum_scatter(tiles, axes[k], scatter_dimension=0, tiled=True)  38.1 us
    psum x4, blocking collectives, one_axis_at_a_time(): return functools.reduce(lax.psum, axes, array)  34.7 us
  transfers between devices with their start and end apart: 3, of which 3 were waited for; matrix products, arithmetic and copies ran while one was open for 0% of the time, Pallas kernels for 0%

commit v1 on v0

v1 whole, which is shorter than its diff:
```python
import functools

import jax
import jax.numpy as jnp
from jax import lax
from jax.experimental import pallas as pl
from jax.experimental.pallas import tpu as pltpu
from jax.sharding import Mesh
from jax.sharding import PartitionSpec as P

F32, BF16, I32 = jnp.float32, jnp.bfloat16, jnp.int32
NT = (((1,), (1,)), ((), ()))
LANES = 128
TILE = 512
CHUNK = 512


def halves(value):
    high = value.astype(BF16)
    return high, (value - high.astype(F32)).astype(BF16)


def thirds(value):
    high = value.astype(BF16)
    rest = value - high.astype(F32)
    middle = rest.astype(BF16)
    return high, middle, (rest - middle.astype(F32)).astype(BF16)


def row_of(ref, start, count):
    return jnp.concatenate([ref[pl.ds(start + k, 1), :] for k in range(count)], axis=1)


def local_kernel(
    offset_ref,
    res_ref,
    cam_ref,
    pt_ref,
    camera_ref,
    slot_ref,
    damp_ref,
    table_ref,
    out_ref,
    sums_ref,
    pos_ref,
    feat_ref,
    point_ref,
    step_ref,
    moved_ref,
    lhs_ref,
):
    n_obs = res_ref.shape[1]
    points = damp_ref.shape[0] * LANES
    tiles = n_obs // TILE

    camera = camera_ref[...]
    high_part, low_part = camera >> 7, camera & 127

    def look_up(k, found):
        line = jnp.broadcast_to(table_ref[pl.ds(k, 1), :], found.shape)
        return jnp.where(high_part == k, jnp.take_along_axis(line, low_part, axis=1), found)

    pos_ref[...] = lax.fori_loop(0, table_ref.shape[0], look_up, jnp.zeros_like(camera), unroll=4)

    point_ref[...] = jnp.zeros_like(point_ref)
    feat_ref[...] = jnp.zeros_like(feat_ref)
    window = lax.broadcasted_iota(I32, (2 * LANES, TILE), 0)

    def tile_onehot(t):
        offset = offset_ref[t]
        index = row_of(slot_ref, t * (TILE // LANES), TILE // LANES) + (offset & 127)
        base = pl.multiple_of((offset >> 7) * LANES, LANES)
        return (window == index).astype(F32).astype(BF16), base

    def add_points(t, _):
        cols = pl.ds(pl.multiple_of(t * TILE, TILE), TILE)
        onehot, base = tile_onehot(t)
        r0, r1 = res_ref[0:1, cols], res_ref[1:2, cols]
        j0, j1 = pt_ref[0, :, cols], pt_ref[1, :, cols]
        feat_ref[0:3, :] = j0 * r0 + j1 * r1
        feat_ref[3:6, :] = j0[0:1] * j0 + j1[0:1] * j1
        feat_ref[6:8, :] = j0[1:2] * j0[1:3] + j1[1:2] * j1[1:3]
        feat_ref[8:9, :] = j0[2:3] * j0[2:3] + j1[2:3] * j1[2:3]
        lhs = jnp.concatenate(thirds(feat_ref[...]), axis=0)
        dots = lax.dot_general(lhs, onehot, NT, preferred_element_type=F32)
        point_ref[:, pl.ds(base, 2 * LANES)] += (dots[32:48] + dots[16:32]) + dots[0:16]
        return 0

    lax.fori_loop(0, tiles, add_points, 0)

    damping = row_of(damp_ref, 0, points // LANES)
    g = [point_ref[k : k + 1, 0:points] for k in range(3)]
    aa, ab, ac, bb, bc, cc = [point_ref[k : k + 1, 0:points] for k in range(3, 9)]
    aa, bb, cc = aa + damping, bb + damping, cc + damping
    cof_aa = bb * cc - bc * bc
    cof_ab = ac * bc - ab * cc
    cof_ac = ab * bc - ac * bb
    cof_bb = aa * cc - ac * ac
    cof_bc = ab * ac - aa * bc
    cof_cc = aa * bb - ab * ab
    determ = aa * cof_aa + ab * cof_ab + ac * cof_ac
    steps = (
        (cof_aa * g[0] + cof_ab * g[1] + cof_ac * g[2]) / determ,
        (cof_ab * g[0] + cof_bb * g[1] + cof_bc * g[2]) / determ,
        (cof_ac * g[0] + cof_bc * g[1] + cof_cc * g[2]) / determ,
    )
    step_ref[...] = jnp.zeros_like(step_ref)
    for k in range(3):
        step_ref[k : k + 1, 0:points] = steps[k]
    point_square = jnp.sum(g[0] * g[0] + g[1] * g[1] + g[2] * g[2])
    residual = res_ref[...]
    cost = jnp.sum(residual * residual)
    lane = lax.broadcasted_iota(I32, sums_ref.shape, 1)
    sums_ref[...] = jnp.where(lane == 0, cost, jnp.where(lane == 1, point_square, 0.0))

    def take_steps(t, _):
        cols = pl.ds(pl.multiple_of(t * TILE, TILE), TILE)
        onehot, base = tile_onehot(t)
        lhs = jnp.concatenate(thirds(step_ref[:, pl.ds(base, 2 * LANES)]), axis=0)
        dots = jnp.dot(lhs, onehot, preferred_element_type=F32)
        step = (dots[16:24] + dots[8:16]) + dots[0:8]
        for a in range(2):
            jac = pt_ref[a, :, cols]
            moved_ref[a : a + 1, cols] = (
                jac[0:1] * step[0:1] + jac[1:2] * step[1:2] + jac[2:3] * step[2:3]
            )
        return 0

    lax.fori_loop(0, tiles, take_steps, 0)

    out_ref[...] = jnp.zeros_like(out_ref)
    hi_iota = lax.broadcasted_iota(I32, (64, CHUNK), 0)
    lo_iota = lax.broadcasted_iota(I32, (256, CHUNK), 0)

    def add_cameras(c, _):
        cols = pl.ds(pl.multiple_of(c * CHUNK, CHUNK), CHUNK)
        pos = row_of(pos_ref, c * (CHUNK // LANES), CHUNK // LANES)
        owner = pos >> 7
        hi = ((owner >> 5) << 4) + (owner & 15)
        lo = (((owner >> 4) & 1) << 7) + (pos & 127)
        hi_hot = (hi_iota == hi).astype(F32).astype(BF16)
        lo_hot = (lo_iota == lo).astype(F32).astype(BF16)
        c0, c1 = cam_ref[0, :, cols], cam_ref[1, :, cols]
        r0, r1 = res_ref[0:1, cols], res_ref[1:2, cols]
        m0, m1 = moved_ref[0:1, cols] - r0, moved_ref[1:2, cols] - r1
        for b, value in enumerate((c0 * r0 + c1 * r1, c0 * m0 + c1 * m1)):
            for p, part in enumerate(halves(value)):
                part = part.astype(F32)
                for m in range(9):
                    line = jnp.broadcast_to(part[m : m + 1], (64, CHUNK)).astype(BF16)
                    row = (b * 9 + m) * 64
                    lhs_ref[row : row + 64, p * CHUNK : (p + 1) * CHUNK] = line * hi_hot
        rhs = jnp.concatenate([lo_hot, lo_hot], axis=1)
        out_ref[...] += lax.dot_general(lhs_ref[...], rhs, NT, preferred_element_type=F32)
        return 0

    lax.fori_loop(0, n_obs // CHUNK, add_cameras, 0)


def local_sums(residual, cam_jacobian, point_jacobian, obs_camera, obs_slot, tile_offset, damping, camera_slot):
    n_obs = residual.shape[1]
    vmem = pl.BlockSpec(memory_space=pltpu.VMEM)
    grid_rows = lambda x: x.reshape(-1, LANES)
    points = damping.shape[0]
    return pl.pallas_call(
        local_kernel,
        out_shape=(
            jax.ShapeDtypeStruct((18 * 64, 256), F32),
            jax.ShapeDtypeStruct((8, LANES), F32),
        ),
        in_specs=[pl.BlockSpec(memory_space=pltpu.SMEM)] + [vmem] * 7,
        out_specs=(vmem, vmem),
        scratch_shapes=[
            pltpu.VMEM((n_obs // LANES, LANES), I32),
            pltpu.VMEM((16, TILE), F32),
            pltpu.VMEM((16, points + LANES), F32),
            pltpu.VMEM((8, points + LANES), F32),
            pltpu.VMEM((2, n_obs), F32),
            pltpu.VMEM((18 * 64, 2 * CHUNK), BF16),
        ],
    )(
        tile_offset,
        residual,
        cam_jacobian,
        point_jacobian,
        grid_rows(obs_camera),
        grid_rows(obs_slot),
        grid_rows(damping),
        grid_rows(camera_slot),
    )


GX_GY = ("gx_0", "gx_1", "gy_0", "gy_1")


def on_device(
    residual, cam_jacobian, point_jacobian, obs_camera, obs_slot, tile_offset, damping, camera_slot
):
    n_obs = residual.shape[1]
    devices = lax.axis_size(GX_GY)
    partial, sums = local_sums(
        residual, cam_jacobian, point_jacobian, obs_camera, obs_slot, tile_offset, damping, camera_slot
    )
    tiles = partial.reshape(18, 4, 16, 2, LANES)
    tiles = jnp.transpose(tiles, (1, 3, 2, 0, 4)).reshape(8, 4, 4, 18, LANES)
    own = lax.psum_scatter(tiles, ("gx_0", "gx_1"), scatter_dimension=0, tiled=False)
    own = lax.psum_scatter(own, "gy_0", scatter_dimension=0, tiled=False)
    own = lax.psum_scatter(own, "gy_1", scatter_dimension=0, tiled=False)
    grad_share, reduced = own[:9], own[9:]
    scalars = jnp.stack([sums[0, 0], sums[0, 1] + jnp.sum(grad_share * grad_share)])
    scalars = lax.psum(scalars, GX_GY)
    cost = scalars[0] / (2.0 * n_obs * devices)
    grad_norm = jnp.sqrt(
        scalars[1] / (9.0 * camera_slot.shape[0] + 3.0 * damping.shape[0] * devices) + 1e-06
    )
    return (reduced, cost, grad_norm)


def solution(mesh):
    finer = Mesh(mesh.devices.reshape(4, 2, 4, 4), GX_GY)
    in_specs = (
        P(None, GX_GY),
        P(None, None, GX_GY),
        P(None, None, GX_GY),
        P(GX_GY),
        P(GX_GY),
        P(GX_GY),
        P(GX_GY),
        P(),
    )
    out_specs = (P(None, GX_GY), P(), P())
    return jax.shard_map(
        on_device, mesh=finer, in_specs=in_specs, out_specs=out_specs, check_vma=False
    )
```

time: 722 us -> 220 us (0.30)
  matrix products: 459 us -> 0 us
  local copies, waits for them, and re-layouts: 99.1 us -> 10.7 us
  Pallas kernels: 0 us -> 49.6 us
  blocking collectives: 48.6 us -> 83 us
  waiting for transfers between devices: 78.5 us -> 54 us
  other arithmetic: 11.5 us -> 2.57 us
    dot_general x48 -> x0, matrix products: 459 us -> none  [the longest x32 395 us: add_block(): jnp.dot(block_values, onehot, precision=lax.Precision.HIGHEST)]
    gather x1 -> x0, local copies, waits for them, and re-layouts: 90.5 us -> none  [on_device(): cam_slots = camera_slot[obs_camera]]
    pallas_call x0 -> x1, Pallas kernels: none -> 49.6 us  [local_sums(): pl.pallas_call(local_kernel, out_shape=(jax.ShapeDtypeStruct((18 * 64, 25...]
    unnamed x4 -> x2, waiting for transfers between devices: 40.4 us -> 0.03 us
    psum x4 -> x1, blocking collectives: 34.7 us -> 68.7 us  [on_device(): scalars = lax.psum(scalars, GX_GY)]
    reduce_scatter x2, waiting for transfers between devices: 38.1 us -> 53.9 us  [the longest x1 33.5 us: on_device(): lax.psum_scatter(tiles, ('gx_0', 'gx_1'), scatter_dimension=0, tiled=False)]
    reduce_sum x7 -> x1, other arithmetic: 10.5 us -> 1.85 us  [on_device(): jnp.sum(grad_share * grad_share)]
  transfers between devices with their start and end apart: 3 -> 2, of which waited for: 3 -> 2; matrix products, arithmetic and copies ran while one was open for 0% -> 1% of each run, Pallas kernels for 0% -> 0%
where the time goes in v1:
time: 220 us; the launch traced here: 219 us
  blocking collectives  83 us (38%)
  waiting for transfers between devices  54 us (25%)
  Pallas kernels  49.6 us (23%)
  between operations  19 us (9%)
  local copies, waits for them, and re-layouts  10.7 us (5%)
  other arithmetic  2.57 us (1%)
    psum x1, blocking collectives, on_device(): scalars = lax.psum(scalars, GX_GY)  68.7 us
    pallas_call x1, Pallas kernels, local_sums(): pl.pallas_call(local_kernel, out_shape=(jax.ShapeDtypeStruct((18 * 64, 25...  49.6 us
    reduce_scatter x1, waiting for transfers between devices, on_device(): lax.psum_scatter(tiles, ('gx_0', 'gx_1'), scatter_dimension=0, tiled=False)  33.5 us
    reduce_scatter x1, waiting for transfers between devices, on_device(): own = lax.psum_scatter(own, 'gy_0', scatter_dimension=0, tiled=False)  20.4 us
    unnamed x1, blocking collectives  14.3 us
    unnamed x7, local copies, waits for them, and re-layouts  5.02 us
  transfers between devices with their start and end apart: 2, of which 2 were waited for; matrix products, arithmetic and copies ran while one was open for 1% of the time, Pallas kernels for 0%

profile of v1, /device:TPU:1, one launch (start us, length us, event | category | flops | bytes accessed | tf_op | source)
XLA Modules:
  0.0 218.9 jit_solution(799112963679150847)
XLA Ops:
  7.2 0.0 copy-start
  7.2 0.0 reduce-scatter.3.cloned.1.call-start
  7.2 3.4 %copy.14.cam_ref = f32[2,9,16384]{2,1,0:T(8,128)} copy(f32[2,9,16384]{2,0,1:T(2,128)} %param.9) | data formatting | bytes 2359296 | tf_op args[1]
  10.6 0.0 copy-done
  10.6 1.1 copy.15.pt_ref
  11.7 49.6 %shard_map.103 = (f32[1152,256]{1,0:T(8,128)}, f32[8,128]{1,0:T(8,128)}) custom-call(s32[32]{0:T(128)} %offset_ref.1, f32[2,16384]{1,0:T(2,128)} %res_ref.1, f32[2,9,16384]{2,1,0:T(8,128)} %copy.14.cam_ref, f32[2,3,16384]{2,1,0:T(4,128)} %copy.15.pt_ref, s32[128,128]{1,0:T(8,128)} %bitcast.19, s32[128,128]{1,0:T(8,128)} %bitcast.20, f32[16,128]{1,0:T(8,128)} %bitcast.23, ...), custom_call_target="tpu_custom_call" | custom-call | tf_op jit(solution)/shard_map/pallas_call | solution.py:165
  61.3 1.9 reshape.38
  63.1 1.9 copy.16
  65.0 0.0 copy-start.1
  65.0 0.0 reduce-scatter.3.cloned.1.call-update
  65.0 0.0 reduce-scatter.5.cloned.1.call-start
  65.1 33.5 %reduce-scatter.3.cloned.1.call-done = f32[1,4,4,18,128]{4,3,2,1,0:T(8,128)} async-done(((f32[8,4,4,18,128]{4,3,2,1,0:T(8,128)}), f32[1,4,4,18,128]{4,3,2,1,0:T(8,128)}) %reduce-scatter.3.cloned.1.call-update) | async-done | bytes 147472 | tf_op jit(solution)/shard_map/reduce_scatter | solution.py:206
  98.6 0.0 reduce-scatter.5.cloned.1.call-update
  98.6 0.0 copy-done.1
  98.7 0.6 dynamic-slice
  99.2 1.4 fusion.1
  100.7 20.4 %reduce-scatter.5.cloned.1.call-done = f32[1,4,18,128]{3,2,1,0:T(8,128)} async-done(((f32[4,4,18,128]{3,2,1,0:T(8,128)}), f32[1,4,18,128]{3,2,1,0:T(8,128)}) %reduce-scatter.5.cloned.1.call-update) | async-done | bytes 36880 | tf_op jit(solution)/shard_map/reduce_scatter | solution.py:207
  121.1 14.3 %all-reduce = f32[4,18,128]{2,1,0:T(8,128)S(1)} all-reduce(f32[4,18,128]{2,1,0:T(8,128)} %bitcast.22), channel_id=4, replica_groups=mesh['gx_0'=4,'gx_1'=2,'gy_0'=4,'gy_1'=4] {'gy_1'}, use_global_device_ids=true, to_apply=%region_2.0.clone | all-reduce | flops 9216 | bytes 73728
  135.4 1.9 fusion
  138.5 0.7 pad_maximum_fusion
  139.2 68.7 %psum.7 = f32[2]{0:T(128)S(1)} all-reduce(f32[2]{0:T(128)S(1)} %pad_maximum_fusion), channel_id=1, replica_groups=mesh['gx_0'=4,'gx_1'=2,'gy_0'=4,'gy_1'=4] {'gx_0','gx_1','gy_0','gy_1'}, use_global_device_ids=true, to_apply=%region_4.0 | all-reduce | flops 2 | bytes 16 | tf_op jit(solution)/shard_map/psum | solution.py:211
  207.9 0.6 fusion.2
Async XLA Ops:
  7.2 3.4 %copy-start = (f32[2,3,16384]{2,0,1:T(2,128)S(1)}, f32[2,3,16384]{2,0,1:T(2,128)}, u32[]{:S(2)}) copy-start(f32[2,3,16384]{2,0,1:T(2,128)} %param.10) | copy-start | bytes 1179652
  7.2 91.4 %reduce-scatter.3.cloned.1.call-start = ((), (), s32[]{:S(2)}) async-start(), calls=%async_computation.2 | async-start | bytes 1769472 | tf_op jit(solution)/shard_map/reduce_scatter | solution.py:206
  65.0 33.6 %copy-start.1 = (u32[128]{0:T(128)S(1)}, u32[128]{0:T(128)}, u32[]{:S(2)}) copy-start(u32[128]{0:T(128)} %constant.16) | copy-start | bytes 1540
  65.0 56.0 %reduce-scatter.5.cloned.1.call-start = ((), (), s32[]{:S(2)}) async-start(), calls=%async_computation.3 | async-start | bytes 245760 | tf_op jit(solution)/shard_map/reduce_scatter | solution.py:207
Sparse Core Ops, SparseCore 0:
  65.2 33.4 reduce-scatter.2
  101.0 20.0 reduce-scatter.4

commit v2 on v1

--- a/solution.py
+++ b/solution.py
@@ -10,6 +10,7 @@
 
 F32, BF16, I32 = jnp.float32, jnp.bfloat16, jnp.int32
 NT = (((1,), (1,)), ((), ()))
+MESH = pl.DeviceIdType.MESH
 LANES = 128
 TILE = 512
 CHUNK = 512
@@ -48,6 +49,7 @@
     step_ref,
     moved_ref,
     lhs_ref,
+    total_ref,
 ):
     n_obs = res_ref.shape[1]
     points = damp_ref.shape[0] * LANES
@@ -128,7 +130,7 @@
 
     lax.fori_loop(0, tiles, take_steps, 0)
 
-    out_ref[...] = jnp.zeros_like(out_ref)
+    total_ref[...] = jnp.zeros_like(total_ref)
     hi_iota = lax.broadcasted_iota(I32, (64, CHUNK), 0)
     lo_iota = lax.broadcasted_iota(I32, (256, CHUNK), 0)
 
@@ -151,10 +153,21 @@
                     row = (b * 9 + m) * 64
                     lhs_ref[row : row + 64, p * CHUNK : (p + 1) * CHUNK] = line * hi_hot
         rhs = jnp.concatenate([lo_hot, lo_hot], axis=1)
-        out_ref[...] += lax.dot_general(lhs_ref[...], rhs, NT, preferred_element_type=F32)
+        dots = lax.dot_general(lhs_ref[...], rhs, NT, preferred_element_type=F32)
+        total_ref[0] += dots[:, :LANES]
+        total_ref[1] += dots[:, LANES:]
         return 0
 
     lax.fori_loop(0, n_obs // CHUNK, add_cameras, 0)
+
+    def regroup(hi, _):
+        for side in range(2):
+            for g in range(3):
+                rows = pl.ds(g * 6 * 64 + hi, 6, stride=64)
+                out_ref[side, g, hi] = total_ref[side, rows, :]
+        return 0
+
+    lax.fori_loop(0, 64, regroup, 0, unroll=4)
 
 
 def local_sums(residual, cam_jacobian, point_jacobian, obs_camera, obs_slot, tile_offset, damping, camera_slot):
@@ -165,7 +178,7 @@
     return pl.pallas_call(
         local_kernel,
         out_shape=(
-            jax.ShapeDtypeStruct((18 * 64, 256), F32),
+            jax.ShapeDtypeStruct((2, 3, 64, 6, LANES), F32),
             jax.ShapeDtypeStruct((8, LANES), F32),
         ),
         in_specs=[pl.BlockSpec(memory_space=pltpu.SMEM)] + [vmem] * 7,
@@ -177,6 +190,7 @@
             pltpu.VMEM((8, points + LANES), F32),
             pltpu.VMEM((2, n_obs), F32),
             pltpu.VMEM((18 * 64, 2 * CHUNK), BF16),
+            pltpu.VMEM((2, 18 * 64, LANES), F32),
         ],
     )(
         tile_offset,
@@ -190,45 +204,232 @@
     )
 
 
-GX_GY = ("gx_0", "gx_1", "gy_0", "gy_1")
+AXES = ("gx_0", "gx_1", "gy_0", "gy_1")
+RINGS = ("gx_0", "gy_0", "gy_1")
+ORDERS = ((0, 1, 2), (1, 2, 0), (2, 0, 1))
+
+
+def neighbours(me, names, sizes):
+    total = 1
+    for name in names:
+        total *= sizes[name]
+    place = 0
+    for name in names:
+        place = place * sizes[name] + me[name]
+    found = []
+    for k in range(1, total):
+        other = lax.rem(place + k, total)
+        target = dict(me)
+        for name in reversed(names):
+            target[name] = lax.rem(other, sizes[name])
+            other = other // sizes[name]
+        found.append(tuple(target[name] for name in AXES))
+    return found
+
+
+def inside(position, index):
+    return (slice(None),) * position + (index,)
+
+
+def exchange_kernel(
+    sizes,
+    scale,
+    part_ref,
+    sums_ref,
+    reduced_ref,
+    cost_ref,
+    norm_ref,
+    pair_ref,
+    whole_ref,
+    in1_ref,
+    sum1_ref,
+    in2_ref,
+    sum2_ref,
+    in3_ref,
+    mine_ref,
+    far_ref,
+    plane_ref,
+    near_ref,
+    pair_send,
+    pair_recv,
+    ring_send,
+    ring_recv,
+    far_send,
+    far_recv,
+    near_send,
+    near_recv,
+):
+    me = {name: lax.axis_index(name) for name in AXES}
+    far = neighbours(me, ("gx_0", "gx_1"), sizes)
+    near = neighbours(me, ("gy_0", "gy_1"), sizes)
+    rings = [neighbours(me, (name,), sizes) for name in RINGS]
+    core = me["gx_1"]
+    partner = (me["gx_0"], 1 - core, me["gy_0"], me["gy_1"])
+
+    barrier = pltpu.get_barrier_semaphore()
+    for target in far + near:
+        pl.semaphore_signal(barrier, inc=1, device_id=target, device_id_type=MESH)
+    pl.semaphore_wait(barrier, len(far) + len(near))
+
+    started = []
+
+    def send(source, target_ref, send_sem, recv_sem, device):
+        copy = pltpu.make_async_remote_copy(
+            src_ref=source,
+            dst_ref=target_ref,
+            send_sem=send_sem,
+            recv_sem=recv_sem,
+            device_id=device,
+            device_id_type=MESH,
+        )
+        copy.start()
+        started.append(copy)
+        return copy
+
+    def spread(source, inbox, group, phase, position):
+        ring = ORDERS[group][phase]
+        name = RINGS[ring]
+        copies = []
+        for k, device in enumerate(rings[ring]):
+            there = device[AXES.index(name)]
+            copies.append(
+                send(
+                    source.at[(group,) + inside(position, there)],
+                    inbox.at[group, k],
+                    ring_send.at[group, phase, k],
+                    ring_recv.at[group, phase, k],
+                    device,
+                )
+            )
+        return copies
+
+    def gather(source, inbox, copies, group, phase, position):
+        for copy in copies:
+            copy.wait_recv()
+        here = me[RINGS[ORDERS[group][phase]]]
+        kept = source[(group,) + inside(position, here)]
+        return (kept + inbox[group, 1]) + (inbox[group, 0] + inbox[group, 2])
+
+    pairs = [
+        send(part_ref.at[1 - core, g], pair_ref.at[g], pair_send.at[g], pair_recv.at[g], partner)
+        for g in range(3)
+    ]
+    first, second, third = [], [], []
+    for g in range(3):
+        pairs[g].wait_recv()
+        whole_ref[g] = part_ref[core, g] + pair_ref[g]
+        first.append(spread(whole_ref, in1_ref, g, 0, ORDERS[g][0]))
+    spots = []
+    for g in range(3):
+        sum1_ref[g] = gather(whole_ref, in1_ref, first[g], g, 0, ORDERS[g][0])
+        left = [d for d in range(3) if d != ORDERS[g][0]]
+        spots.append(left.index(ORDERS[g][1]))
+        second.append(spread(sum1_ref, in2_ref, g, 1, spots[g]))
+    for g in range(3):
+        sum2_ref[g] = gather(sum1_ref, in2_ref, second[g], g, 1, spots[g])
+        third.append(spread(sum2_ref, in3_ref, g, 2, 0))
+    own = [gather(sum2_ref, in3_ref, third[g], g, 2, 0) for g in range(3)]
+
+    rows = jnp.concatenate(own, axis=0)
+    half = rows.shape[0] // 2
+    reduced_ref[...] = rows[half:]
+    camera_square = jnp.sum(rows[:half] * rows[:half])
+    lane = lax.broadcasted_iota(I32, mine_ref.shape, 1)
+    mine_ref[...] = sums_ref[...] + jnp.where(lane == 1, camera_square, 0.0)
+    arrivals = [
+        send(mine_ref, far_ref.at[k], far_send.at[k], far_recv.at[k], device)
+        for k, device in enumerate(far)
+    ]
+    for copy in arrivals:
+        copy.wait_recv()
+    plane_ref[...] = mine_ref[...] + jnp.sum(far_ref[...], axis=0)
+    arrivals = [
+        send(plane_ref, near_ref.at[k], near_send.at[k], near_recv.at[k], device)
+        for k, device in enumerate(near)
+    ]
+    for copy in arrivals:
+        copy.wait_recv()
+    totals = plane_ref[...] + jnp.sum(near_ref[...], axis=0)
+    first_row = lax.broadcasted_iota(I32, mine_ref.shape, 0) == 0
+    cost = totals / scale[0]
+    norm = jnp.sqrt(totals / scale[1] + 1e-06)
+    cost_ref[0, 0] = jnp.sum(jnp.where(first_row & (lane == 0), cost, 0.0))
+    norm_ref[0, 0] = jnp.sum(jnp.where(first_row & (lane == 1), norm, 0.0))
+    for copy in started:
+        copy.wait_send()
+
+
+def exchange(partial, sums, sizes, scale):
+    rows = partial.shape[-2]
+    block = (rows, LANES)
+    vmem = pl.BlockSpec(memory_space=pltpu.VMEM)
+    smem = pl.BlockSpec(memory_space=pltpu.SMEM)
+    buffer = lambda *lead: pltpu.VMEM(lead + block, F32)
+    dma = pltpu.SemaphoreType.DMA
+    far = sizes["gx_0"] * sizes["gx_1"] - 1
+    near = sizes["gy_0"] * sizes["gy_1"] - 1
+    return pl.pallas_call(
+        functools.partial(exchange_kernel, sizes, scale),
+        out_shape=(
+            jax.ShapeDtypeStruct((3 * rows // 2, LANES), F32),
+            jax.ShapeDtypeStruct((1, 1), F32),
+            jax.ShapeDtypeStruct((1, 1), F32),
+        ),
+        in_specs=[vmem, vmem],
+        out_specs=(vmem, smem, smem),
+        scratch_shapes=[
+            buffer(3, 4, 4, 4),
+            buffer(3, 4, 4, 4),
+            buffer(3, 3, 4, 4),
+            buffer(3, 4, 4),
+            buffer(3, 3, 4),
+            buffer(3, 4),
+            buffer(3, 3),
+            pltpu.VMEM((8, LANES), F32),
+            pltpu.VMEM((far, 8, LANES), F32),
+            pltpu.VMEM((8, LANES), F32),
+            pltpu.VMEM((near, 8, LANES), F32),
+            dma((3,)),
+            dma((3,)),
+            dma((3, 3, 3)),
+            dma((3, 3, 3)),
+            dma((far,)),
+            dma((far,)),
+            dma((near,)),
+            dma((near,)),
+        ],
+        compiler_params=pltpu.CompilerParams(collective_id=0, has_side_effects=True),
+    )(partial, sums)
 
 
 def on_device(
     residual, cam_jacobian, point_jacobian, obs_camera, obs_slot, tile_offset, damping, camera_slot
 ):
     n_obs = residual.shape[1]
-    devices = lax.axis_size(GX_GY)
+    sizes = {name: lax.axis_size(name) for name in AXES}
+    devices = lax.axis_size(AXES)
     partial, sums = local_sums(
         residual, cam_jacobian, point_jacobian, obs_camera, obs_slot, tile_offset, damping, camera_slot
     )
-    tiles = partial.reshape(18, 4, 16, 2, LANES)
-    tiles = jnp.transpose(tiles, (1, 3, 2, 0, 4)).reshape(8, 4, 4, 18, LANES)
-    own = lax.psum_scatter(tiles, ("gx_0", "gx_1"), scatter_dimension=0, tiled=False)
-    own = lax.psum_scatter(own, "gy_0", scatter_dimension=0, tiled=False)
-    own = lax.psum_scatter(own, "gy_1", scatter_dimension=0, tiled=False)
-    grad_share, reduced = own[:9], own[9:]
-    scalars = jnp.stack([sums[0, 0], sums[0, 1] + jnp.sum(grad_share * grad_share)])
-    scalars = lax.psum(scalars, GX_GY)
-    cost = scalars[0] / (2.0 * n_obs * devices)
-    grad_norm = jnp.sqrt(
-        scalars[1] / (9.0 * camera_slot.shape[0] + 3.0 * damping.shape[0] * devices) + 1e-06
-    )
-    return (reduced, cost, grad_norm)
+    partial = partial.reshape(2, 3, 4, 4, 4, 6, LANES)
+    scale = (2.0 * n_obs * devices, 9.0 * camera_slot.shape[0] + 3.0 * damping.shape[0] * devices)
+    reduced, cost, grad_norm = exchange(partial, sums, sizes, scale)
+    return (reduced, cost.reshape(()), grad_norm.reshape(()))
 
 
 def solution(mesh):
-    finer = Mesh(mesh.devices.reshape(4, 2, 4, 4), GX_GY)
+    finer = Mesh(mesh.devices.reshape(4, 2, 4, 4), AXES)
     in_specs = (
-        P(None, GX_GY),
-        P(None, None, GX_GY),
-        P(None, None, GX_GY),
-        P(GX_GY),
-        P(GX_GY),
-        P(GX_GY),
-        P(GX_GY),
+        P(None, AXES),
+        P(None, None, AXES),
+        P(None, None, AXES),
+        P(AXES),
+        P(AXES),
+        P(AXES),
+        P(AXES),
         P(),
     )
-    out_specs = (P(None, GX_GY), P(), P())
+    out_specs = (P(None, AXES), P(), P())
     return jax.shard_map(
         on_device, mesh=finer, in_specs=in_specs, out_specs=out_specs, check_vma=False
     )

time: 220 us -> 94 us (0.43)
  blocking collectives: 83 us -> 0 us
  waiting for transfers between devices: 54 us -> 0 us
  Pallas kernels: 49.6 us -> 82.8 us
  between operations: 19 us -> 4.14 us
  local copies, waits for them, and re-layouts: 10.7 us -> 6.69 us
  other arithmetic: 2.57 us -> 0 us
    psum x1 -> x0, blocking collectives: 68.7 us -> none  [on_device(): scalars = lax.psum(scalars, GX_GY)]
    reduce_scatter x2 -> x0, waiting for transfers between devices: 53.9 us -> none  [the longest x1 33.5 us: on_device(): lax.psum_scatter(tiles, ('gx_0', 'gx_1'), scatter_dimension=0, tiled=False)]
    pallas_call x1 -> x2, Pallas kernels: 49.6 us -> 82.8 us  [the longest x1 50.6 us: local_sums(): pl.pallas_call(local_kernel, out_shape=(jax.ShapeDtypeStruct((2, 3, 64, 6...]
    unnamed x1 -> x0, blocking collectives: 14.3 us -> none
    unnamed x7 -> x3, local copies, waits for them, and re-layouts: 5.02 us -> 6.69 us
  transfers between devices with their start and end apart: 2 -> 0, of which waited for: 2 -> 0; matrix products, arithmetic and copies ran while one was open for 1% -> 0% of each run, Pallas kernels for 0% -> 0%
where the time goes in v2:
time: 94 us; the launch traced here: 93.6 us
  Pallas kernels  82.8 us (88%)
  local copies, waits for them, and re-layouts  6.69 us (7%)
  between operations  4.14 us (4%)
    pallas_call x1, Pallas kernels, local_sums(): pl.pallas_call(local_kernel, out_shape=(jax.ShapeDtypeStruct((2, 3, 64, 6...  50.6 us
    pallas_call x1, Pallas kernels, exchange(): pl.pallas_call(functools.partial(exchange_kernel, sizes, scale), out_shap...  32.3 us
    unnamed x3, local copies, waits for them, and re-layouts  6.69 us

profile of v2, /device:TPU:1, one launch (start us, length us, event | category | flops | bytes accessed | tf_op | source)
XLA Modules:
  0.0 93.6 jit_solution(16282634493468458718)
XLA Ops:
  0.6 2.1 %copy.12.pt_ref = f32[2,3,16384]{2,1,0:T(4,128)} copy(f32[2,3,16384]{2,0,1:T(2,128)} %param.10) | data formatting | bytes 786432 | tf_op args[2]
  2.7 3.3 %copy.11.cam_ref = f32[2,9,16384]{2,1,0:T(8,128)} copy(f32[2,9,16384]{2,0,1:T(2,128)} %param.9) | data formatting | bytes 2359296 | tf_op args[1]
  6.0 50.6 %shard_map.103 = (f32[2,3,64,6,128]{4,3,2,1,0:T(8,128)}, f32[8,128]{1,0:T(8,128)}) custom-call(s32[32]{0:T(128)} %offset_ref.1, f32[2,16384]{1,0:T(2,128)} %res_ref.1, f32[2,9,16384]{2,1,0:T(8,128)} %copy.11.cam_ref, f32[2,3,16384]{2,1,0:T(4,128)} %copy.12.pt_ref, s32[128,128]{1,0:T(8,128)} %bitcast.8, s32[128,128]{1,0:T(8,128)} %bitcast.9, ...), custom_call_target="tpu_custom_call" | custom-call | tf_op jit(solution)/shard_map/pallas_call | solution.py:178
  56.6 32.3 %shard_map.104 = (f32[9,128]{1,0:T(8,128)}, f32[1,1]{1,0:T(1,128)}, f32[1,1]{1,0:T(1,128)}) custom-call(f32[2,3,4,4,4,6,128]{6,5,4,3,2,1,0:T(8,128)} %bitcast.7, f32[8,128]{1,0:T(8,128)} %get-tuple-element.9.sums_ref), custom_call_target="tpu_custom_call" | custom-call | tf_op jit(solution)/shard_map/pallas_call | solution.py:371
  88.8 1.3 %copy.16 = f32[9,128]{1,0:T(8,128)} copy(f32[9,128]{1,0:T(8,128)} %get-tuple-element.16) | data formatting | bytes 9216

commit v3 on v2

v3 whole, which is shorter than its diff:
```python
import functools

import jax
import jax.numpy as jnp
from jax import lax
from jax.experimental import pallas as pl
from jax.experimental.pallas import tpu as pltpu
from jax.sharding import Mesh
from jax.sharding import PartitionSpec as P

F32, BF16, I32 = jnp.float32, jnp.bfloat16, jnp.int32
NT = (((1,), (1,)), ((), ()))
MESH = pl.DeviceIdType.MESH
LANES = 128
CAM = 9
BINS = 64


def thirds(value):
    high = value.astype(BF16)
    rest = value - high.astype(F32)
    middle = rest.astype(BF16)
    return high, middle, (rest - middle.astype(F32)).astype(BF16)


def row_of(ref, start, count):
    return jnp.concatenate([ref[pl.ds(start + k, 1), :] for k in range(count)], axis=1)


def pair_sum(product):
    return product + pltpu.roll(product, product.shape[0] - 1, 0)


def window_base(offset):
    return pl.multiple_of((offset >> 7) * LANES, LANES)


def one_hot(count, index):
    shape = (count, index.shape[1])
    return (lax.broadcasted_iota(I32, shape, 0) == index).astype(F32).astype(BF16)


def push_bins(tile, pos_ref):
    for unit in range(2):
        pos = row_of(pos_ref, tile * 4 + unit * 2, 2)
        lo = (((pos >> 11) & 1) << 7) + (pos & 127)
        pltpu.matmul_push_rhs(one_hot(2 * LANES, lo), 0, unit, transpose=True)


def split_lines(tile, factor, cam_ref, line_ref):
    rows = pl.ds(pl.multiple_of(tile * 8, 8), 8)
    for m in range(CAM):
        value = pair_sum(cam_ref[m, rows, :] * factor)
        high = value.astype(BF16).astype(F32)
        line_ref[0, m] = high
        line_ref[1, m] = value - high


def add_lines(tile, pos_ref, line_ref, accs):
    hots = []
    for unit in range(2):
        owner = row_of(pos_ref, tile * 4 + unit * 2, 2) >> 7
        hots.append(one_hot(BINS, ((owner >> 5) << 4) + (owner & 15)))
    for part in range(2):
        for m in range(CAM):
            for unit in range(2):
                pieces = []
                for q in range(2):
                    row = 2 * (2 * unit + q)
                    line = jnp.broadcast_to(line_ref[part, m, row : row + 1], (16, LANES)).astype(BF16)
                    hot = hots[unit][:, q * LANES : (q + 1) * LANES].reshape(BINS // 16, 16, LANES)
                    pieces.append((hot * line[None]).reshape(BINS, LANES))
                lhs = jnp.concatenate(pieces, axis=1)
                staged = 0 if part == 0 and m == 0 else None
                pltpu.matmul_acc_lhs(accs[unit * CAM + m], lhs, staged)


def empty_accs(accs):
    return [pltpu.matmul_pop(acc) for acc in accs]


def drain(accs, total_ref):
    for unit in range(2):
        pltpu.matmul_acc_lhs(accs[unit * CAM], jnp.zeros((BINS, 2 * LANES), BF16), 0)
    for m in range(CAM):
        total = pltpu.matmul_pop(accs[m]) + pltpu.matmul_pop(accs[CAM + m])
        total_ref[0, m * BINS : (m + 1) * BINS] = total[:, :LANES]
        total_ref[1, m * BINS : (m + 1) * BINS] = total[:, LANES:]


def regroup_into(out_ref, total_ref):
    def one(hi, _):
        for side in range(2):
            for g in range(3):
                rows = pl.ds(g * 3 * BINS + hi, 3, stride=BINS)
                out_ref[side, g, hi >> 4, (hi >> 2) & 3, hi & 3] = total_ref[side, rows, :]
        return 0

    lax.fori_loop(0, BINS, one, 0, unroll=4)


def solve_points(point_ref, damp_ref, step_ref):
    points = damp_ref.shape[0] * LANES
    damping = row_of(damp_ref, 0, points // LANES)
    g = [point_ref[k : k + 1, 0:points] for k in range(3)]
    aa, ab, ac, bb, bc, cc = [point_ref[k : k + 1, 0:points] for k in range(3, 9)]
    aa, bb, cc = aa + damping, bb + damping, cc + damping
    cof_aa = bb * cc - bc * bc
    cof_ab = ac * bc - ab * cc
    cof_ac = ab * bc - ac * bb
    cof_bb = aa * cc - ac * ac
    cof_bc = ab * ac - aa * bc
    cof_cc = aa * bb - ab * ab
    determ = aa * cof_aa + ab * cof_ab + ac * cof_ac
    steps = [
        (cof_aa * g[0] + cof_ab * g[1] + cof_ac * g[2]) / determ,
        (cof_ab * g[0] + cof_bb * g[1] + cof_bc * g[2]) / determ,
        (cof_ac * g[0] + cof_bc * g[1] + cof_cc * g[2]) / determ,
    ]
    step_ref[...] = jnp.zeros_like(step_ref)
    for k in range(3):
        for p, part in enumerate(thirds(steps[k])):
            step_ref[3 * p + k : 3 * p + k + 1, 0:points] = part.astype(F32)
    return jnp.sum(g[0] * g[0] + g[1] * g[1] + g[2] * g[2])


def first_kernel(
    offset_ref,
    res_ref,
    cam_ref,
    pt_ref,
    camera_ref,
    slot_ref,
    damp_ref,
    table_ref,
    grad_ref,
    pos_ref,
    index_ref,
    window_ref,
    sums_ref,
    step_ref,
    feat_ref,
    point_ref,
    line_ref,
    total_ref,
    *accs,
):
    tiles = res_ref.shape[0] // 8
    point_accs, accs = accs[:2], accs[2:]
    point_ref[...] = jnp.zeros_like(point_ref)
    feat_ref[...] = jnp.zeros_like(feat_ref)
    empty_accs(point_accs + accs)

    def find(tile):
        lines = pl.ds(pl.multiple_of(tile * 4, 4), 4)
        camera = camera_ref[lines, :]
        high, low = camera >> 7, camera & 127
        found = [jnp.zeros_like(camera)] * 4
        for k in range(table_ref.shape[0]):
            line = jnp.broadcast_to(table_ref[k : k + 1, :], camera.shape)
            taken = jnp.take_along_axis(line, low, axis=1, mode="promise_in_bounds")
            found[k % 4] = jnp.where(high == k, taken, found[k % 4])
        pos_ref[lines, :] = (found[0] + found[1]) + (found[2] + found[3])

    def residual_of(tile):
        return res_ref[pl.ds(pl.multiple_of(tile * 8, 8), 8), :]

    def add_points(tile):
        rows = pl.ds(pl.multiple_of(tile * 8, 8), 8)
        r = residual_of(tile)
        j = [pt_ref[k, rows, :] for k in range(3)]
        products = [j[0] * r, j[1] * r, j[2] * r]
        products += [j[0] * j[0], j[0] * j[1], j[0] * j[2]]
        products += [j[1] * j[1], j[1] * j[2], j[2] * j[2]]
        for f, product in enumerate(products):
            feat_ref[f * 8 : f * 8 + 8, :] = pair_sum(product)
        offset = offset_ref[tile]
        lines = pl.ds(pl.multiple_of(tile * 4, 4), 4)
        index_ref[lines, :] = slot_ref[lines, :] + (offset & 127)
        index, base = row_of(index_ref, tile * 4, 4), window_base(offset)
        for unit in range(2):
            columns = [feat_ref[pl.ds(4 * unit + 2 * q, 16, stride=8), :] for q in range(2)]
            lhs = jnp.concatenate(thirds(jnp.concatenate(columns, axis=1)), axis=0)
            hot = one_hot(2 * LANES, index[:, unit * 2 * LANES : (unit + 1) * 2 * LANES])
            pltpu.matmul_push_rhs(hot, 1, unit, transpose=True)
            pltpu.matmul_acc_lhs(point_accs[unit], lhs, 1)
        return base

    find(0)
    push_bins(0, pos_ref)
    split_lines(0, residual_of(0), cam_ref, line_ref.at[0])

    def one_tile(tile, now, later):
        ahead = jnp.minimum(tile + 1, tiles - 1)
        add_lines(tile, pos_ref, line_ref.at[now], accs)
        base = add_points(tile)
        find(ahead)
        push_bins(ahead, pos_ref)
        split_lines(ahead, residual_of(ahead), cam_ref, line_ref.at[later])
        dots = pltpu.matmul_pop(point_accs[0]) + pltpu.matmul_pop(point_accs[1])
        point_ref[:, pl.ds(base, 2 * LANES)] += (dots[32:48] + dots[16:32]) + dots[0:16]

    def two_tiles(k, _):
        one_tile(2 * k, 0, 1)
        one_tile(2 * k + 1, 1, 0)
        return 0

    lax.fori_loop(0, tiles // 2, two_tiles, 0)
    drain(accs, total_ref)
    regroup_into(grad_ref, total_ref)
    point_square = solve_points(point_ref, damp_ref, step_ref)

    def cut_window(tile, _):
        window_ref[tile] = step_ref[:, pl.ds(window_base(offset_ref[tile]), 2 * LANES)].astype(BF16)
        return 0

    lax.fori_loop(0, tiles, cut_window, 0, unroll=4)
    residual = res_ref[...]
    cost = jnp.sum(residual * residual)
    lane = lax.broadcasted_iota(I32, sums_ref.shape, 1)
    sums_ref[...] = jnp.where(lane == 0, cost, jnp.where(lane == 1, point_square, 0.0))


def move_start(tile, index_ref, window_ref, point_accs):
    index = row_of(index_ref, tile * 4, 4)
    lhs = window_ref[tile]
    for unit in range(2):
        hot = one_hot(2 * LANES, index[:, unit * 2 * LANES : (unit + 1) * 2 * LANES])
        pltpu.matmul_push_rhs(hot, 1, unit)
        pltpu.matmul_acc_lhs(point_accs[unit], lhs, 1)


def move_end(tile, pt_ref, res_ref, moved_ref, point_accs):
    for unit in range(2):
        dots = pltpu.matmul_pop(point_accs[unit])
        taken = (dots[6:9] + dots[3:6]) + dots[0:3]
        for q in range(2):
            piece = taken[:, q * LANES : (q + 1) * LANES]
            for a in range(2):
                row = tile * 8 + 2 * (2 * unit + q) + a
                jac = jnp.concatenate([pt_ref[k, pl.ds(row, 1), :] for k in range(3)], axis=0)
                moved = jnp.sum(jac * piece, axis=0, keepdims=True)
                moved_ref[pl.ds(row, 1), :] = moved - res_ref[pl.ds(row, 1), :]


def second_start(index_ref, window_ref, pt_ref, res_ref, moved_ref, pos_ref, cam_ref, line_ref, accs):
    point_accs, accs = accs[:2], accs[2:]
    empty_accs(point_accs + accs)
    for tile in range(2):
        move_start(tile, index_ref, window_ref, point_accs)
        move_end(tile, pt_ref, res_ref, moved_ref, point_accs)
    push_bins(0, pos_ref)
    split_lines(0, moved_ref[0:8, :], cam_ref, line_ref.at[0])


def second_tiles(
    first, last, index_ref, window_ref, pt_ref, res_ref, moved_ref, pos_ref, cam_ref, line_ref, accs
):
    tiles = res_ref.shape[0] // 8
    point_accs, accs = accs[:2], accs[2:]

    def one_tile(tile, now, later):
        ahead = jnp.minimum(tile + 1, tiles - 1)
        after = jnp.minimum(tile + 2, tiles - 1)
        add_lines(tile, pos_ref, line_ref.at[now], accs)
        move_start(after, index_ref, window_ref, point_accs)
        push_bins(ahead, pos_ref)
        factor = moved_ref[pl.ds(pl.multiple_of(ahead * 8, 8), 8), :]
        split_lines(ahead, factor, cam_ref, line_ref.at[later])
        move_end(after, pt_ref, res_ref, moved_ref, point_accs)

    def two_tiles(k, _):
        one_tile(2 * k, 0, 1)
        one_tile(2 * k + 1, 1, 0)
        return 0

    lax.fori_loop(first // 2, last // 2, two_tiles, 0)


def scoped(kernel, shapes):
    def whole(*refs):
        pl.run_scoped(lambda *accs: kernel(*refs, *accs), *shapes())

    return whole


def acc_shapes():
    points = [pltpu.ACC(unit)((48, 2 * LANES), F32) for unit in range(2)]
    return points + [pltpu.ACC(unit)((BINS, 2 * LANES), F32) for unit in range(2) for _ in range(CAM)]


def take_shapes():
    points = [pltpu.ACC(unit)((16, 2 * LANES), F32) for unit in range(2)]
    return points + acc_shapes()[2:]


def row_major(array):
    rows, n_obs = array.shape[1:-1], array.shape[-1]
    blocks = array.reshape(2, *rows, n_obs // LANES, LANES)
    blocks = jnp.moveaxis(blocks, 0, -2)
    return blocks.reshape(*rows, 2 * n_obs // LANES, LANES)


def first_half(residual, cam_jacobian, point_jacobian, obs_camera, obs_slot, tile_offset, damping, camera_slot):
    vmem = pl.BlockSpec(memory_space=pltpu.VMEM)
    points = damping.shape[0]
    return pl.pallas_call(
        scoped(first_kernel, acc_shapes),
        out_shape=(
            jax.ShapeDtypeStruct((2, 3, 4, 4, 4, 3, LANES), F32),
            jax.ShapeDtypeStruct(obs_camera.shape, I32),
            jax.ShapeDtypeStruct(obs_camera.shape, I32),
            jax.ShapeDtypeStruct((tile_offset.size, 16, 2 * LANES), BF16),
            jax.ShapeDtypeStruct((8, LANES), F32),
        ),
        in_specs=[pl.BlockSpec(memory_space=pltpu.SMEM)] + [vmem] * 7,
        out_specs=(vmem,) * 5,
        scratch_shapes=[
            pltpu.VMEM((16, damping.size + LANES), F32),
            pltpu.VMEM((16 * 8, LANES), F32),
            pltpu.VMEM((16, damping.size + LANES), F32),
            pltpu.VMEM((2, 2, CAM, 8, LANES), F32),
            pltpu.VMEM((2, CAM * BINS, LANES), F32),
        ],
    )(tile_offset, residual, cam_jacobian, point_jacobian, obs_camera, obs_slot, damping, camera_slot)


AXES = ("gx_0", "gx_1", "gy_0", "gy_1")
RINGS = ("gx_0", "gy_0", "gy_1")
ORDERS = ((0, 1, 2), (1, 2, 0), (2, 0, 1))
SPOTS = (0, 1, 0)


def neighbours(me, names, sizes):
    total = 1
    for name in names:
        total *= sizes[name]
    place = 0
    for name in names:
        place = place * sizes[name] + me[name]
    found = []
    for k in range(1, total):
        other = lax.rem(place + k, total)
        target = dict(me)
        for name in reversed(names):
            target[name] = lax.rem(other, sizes[name])
            other = other // sizes[name]
        found.append(tuple(target[name] for name in AXES))
    return found


def inside(position, index):
    return (slice(None),) * position + (index,)


def second_kernel(
    sizes,
    scale,
    res_ref,
    cam_ref,
    pt_ref,
    pos_ref,
    index_ref,
    window_ref,
    grad_ref,
    sums_ref,
    reduced_ref,
    cost_ref,
    norm_ref,
    moved_ref,
    line_ref,
    total_ref,
    move_ref,
    pair_ref,
    whole_ref,
    in1_ref,
    sum1_ref,
    in2_ref,
    sum2_ref,
    in3_ref,
    mine_ref,
    far_ref,
    plane_ref,
    near_ref,
    pair_send,
    pair_recv,
    ring_send,
    ring_recv,
    far_send,
    far_recv,
    near_send,
    near_recv,
    *accs,
):
    me = {name: lax.axis_index(name) for name in AXES}
    far = neighbours(me, ("gx_0", "gx_1"), sizes)
    near = neighbours(me, ("gy_0", "gy_1"), sizes)
    rings = [neighbours(me, (name,), sizes) for name in RINGS]
    core = me["gx_1"]
    partner = (me["gx_0"], 1 - core, me["gy_0"], me["gy_1"])

    barrier = pltpu.get_barrier_semaphore()
    for target in far + near:
        pl.semaphore_signal(barrier, inc=1, device_id=target, device_id_type=MESH)

    started = []

    def send(source, target_ref, send_sem, recv_sem, device):
        copy = pltpu.make_async_remote_copy(
            src_ref=source,
            dst_ref=target_ref,
            send_sem=send_sem,
            recv_sem=recv_sem,
            device_id=device,
            device_id_type=MESH,
        )
        copy.start()
        started.append(copy)
        return copy

    def spread(source, inbox, job, group, phase, position):
        ring = ORDERS[group][phase]
        name = RINGS[ring]
        copies = []
        for k, device in enumerate(rings[ring]):
            there = device[AXES.index(name)]
            copies.append(
                send(
                    source.at[(job, group) + inside(position, there)],
                    inbox.at[job, group, k],
                    ring_send.at[job, group, phase, k],
                    ring_recv.at[job, group, phase, k],
                    device,
                )
            )
        return copies

    def gather(source, inbox, copies, job, group, phase, position):
        for copy in copies:
            copy.wait_recv()
        here = me[RINGS[ORDERS[group][phase]]]
        kept = source[(job, group) + inside(position, here)]
        return (kept + inbox[job, group, 1]) + (inbox[job, group, 0] + inbox[job, group, 2])

    flight = {}

    def pairs(job, source):
        flight[job] = [
            send(
                source.at[1 - core, g],
                pair_ref.at[job, g],
                pair_send.at[job, g],
                pair_recv.at[job, g],
                partner,
            )
            for g in range(3)
        ]

    def phase_one(job, source):
        copies = flight[job]
        flight[job] = []
        for g in range(3):
            copies[g].wait_recv()
            whole_ref[job, g] = source[core, g] + pair_ref[job, g]
            flight[job].append(spread(whole_ref, in1_ref, job, g, 0, ORDERS[g][0]))

    def phase_two(job):
        copies = flight[job]
        flight[job] = []
        for g in range(3):
            sum1_ref[job, g] = gather(whole_ref, in1_ref, copies[g], job, g, 0, ORDERS[g][0])
            flight[job].append(spread(sum1_ref, in2_ref, job, g, 1, SPOTS[g]))

    def phase_three(job):
        copies = flight[job]
        flight[job] = []
        for g in range(3):
            sum2_ref[job, g] = gather(sum1_ref, in2_ref, copies[g], job, g, 1, SPOTS[g])
            flight[job].append(spread(sum2_ref, in3_ref, job, g, 2, 0))

    def finish(job):
        own = [gather(sum2_ref, in3_ref, flight[job][g], job, g, 2, 0) for g in range(3)]
        return jnp.concatenate(own, axis=0)

    refs = (index_ref, window_ref, pt_ref, res_ref, moved_ref, pos_ref, cam_ref, line_ref, accs)
    second_start(*refs)
    pl.semaphore_wait(barrier, len(far) + len(near))
    pairs(0, grad_ref)
    second_tiles(0, 4, *refs)
    phase_one(0, grad_ref)
    second_tiles(4, 12, *refs)
    phase_two(0)
    second_tiles(12, 18, *refs)
    phase_three(0)
    second_tiles(18, 24, *refs)
    grads = finish(0)
    lane = lax.broadcasted_iota(I32, mine_ref.shape, 1)
    mine_ref[...] = sums_ref[...] + jnp.where(lane == 1, jnp.sum(grads * grads), 0.0)
    arrivals = [
        send(mine_ref, far_ref.at[k], far_send.at[k], far_recv.at[k], device)
        for k, device in enumerate(far)
    ]
    second_tiles(24, 32, *refs)
    drain(accs[2:], total_ref)
    regroup_into(move_ref, total_ref)
    pairs(1, move_ref)
    for copy in arrivals:
        copy.wait_recv()
    plane_ref[...] = mine_ref[...] + jnp.sum(far_ref[...], axis=0)
    phase_one(1, move_ref)
    arrivals = [
        send(plane_ref, near_ref.at[k], near_send.at[k], near_recv.at[k], device)
        for k, device in enumerate(near)
    ]
    phase_two(1)
    phase_three(1)
    for copy in arrivals:
        copy.wait_recv()
    totals = plane_ref[...] + jnp.sum(near_ref[...], axis=0)
    first_row = lax.broadcasted_iota(I32, mine_ref.shape, 0) == 0
    cost = totals / scale[0]
    norm = jnp.sqrt(totals / scale[1] + 1e-06)
    cost_ref[0, 0] = jnp.sum(jnp.where(first_row & (lane == 0), cost, 0.0))
    norm_ref[0, 0] = jnp.sum(jnp.where(first_row & (lane == 1), norm, 0.0))
    reduced_ref[...] = finish(1)
    for copy in started:
        copy.wait_send()


def second_half(residual, cam_jacobian, point_jacobian, pos, index, window, grad, sums, sizes, scale):
    vmem = pl.BlockSpec(memory_space=pltpu.VMEM)
    smem = pl.BlockSpec(memory_space=pltpu.SMEM)
    rows = CAM // 3
    buffer = lambda *lead: pltpu.VMEM(lead + (rows, LANES), F32)
    dma = pltpu.SemaphoreType.DMA
    far = sizes["gx_0"] * sizes["gx_1"] - 1
    near = sizes["gy_0"] * sizes["gy_1"] - 1
    return pl.pallas_call(
        scoped(functools.partial(second_kernel, sizes, scale), take_shapes),
        out_shape=(
            jax.ShapeDtypeStruct((CAM, LANES), F32),
            jax.ShapeDtypeStruct((1, 1), F32),
            jax.ShapeDtypeStruct((1, 1), F32),
        ),
        in_specs=[vmem] * 8,
        out_specs=(vmem, smem, smem),
        scratch_shapes=[
            pltpu.VMEM(residual.shape, F32),
            pltpu.VMEM((2, 2, CAM, 8, LANES), F32),
            pltpu.VMEM((2, CAM * BINS, LANES), F32),
            buffer(2, 3, 4, 4, 4),
            buffer(2, 3, 4, 4, 4),
            buffer(2, 3, 4, 4, 4),
            buffer(2, 3, 3, 4, 4),
            buffer(2, 3, 4, 4),
            buffer(2, 3, 3, 4),
            buffer(2, 3, 4),
            buffer(2, 3, 3),
            pltpu.VMEM((8, LANES), F32),
            pltpu.VMEM((far, 8, LANES), F32),
            pltpu.VMEM((8, LANES), F32),
            pltpu.VMEM((near, 8, LANES), F32),
            dma((2, 3)),
            dma((2, 3)),
            dma((2, 3, 3, 3)),
            dma((2, 3, 3, 3)),
            dma((far,)),
            dma((far,)),
            dma((near,)),
            dma((near,)),
        ],
        compiler_params=pltpu.CompilerParams(collective_id=0, has_side_effects=True),
    )(residual, cam_jacobian, point_jacobian, pos, index, window, grad, sums)


def on_device(
    residual, cam_jacobian, point_jacobian, obs_camera, obs_slot, tile_offset, damping, camera_slot
):
    n_obs = residual.shape[1]
    sizes = {name: lax.axis_size(name) for name in AXES}
    devices = lax.axis_size(AXES)
    scale = (2.0 * n_obs * devices, 9.0 * camera_slot.shape[0] + 3.0 * damping.shape[0] * devices)
    lines = lambda array: array.reshape(-1, LANES)
    res, cam, pt = row_major(residual), row_major(cam_jacobian), row_major(point_jacobian)
    grad, pos, index, window, sums = first_half(
        res, cam, pt, lines(obs_camera), lines(obs_slot), tile_offset, lines(damping), lines(camera_slot)
    )
    reduced, cost, norm = second_half(res, cam, pt, pos, index, window, grad, sums, sizes, scale)
    return (reduced, cost.reshape(()), norm.reshape(()))


def solution(mesh):
    finer = Mesh(mesh.devices.reshape(4, 2, 4, 4), AXES)
    in_specs = (
        P(None, AXES),
        P(None, None, AXES),
        P(None, None, AXES),
        P(AXES),
        P(AXES),
        P(AXES),
        P(AXES),
        P(),
    )
    out_specs = (P(None, AXES), P(), P())
    return jax.shard_map(
        on_device, mesh=finer, in_specs=in_specs, out_specs=out_specs, check_vma=False
    )
```

time: 94 us -> 61.6 us (0.66)
  Pallas kernels: 82.8 us -> 55.9 us
  local copies, waits for them, and re-layouts: 6.69 us -> 1.3 us
    pallas_call x2, Pallas kernels: 82.8 us -> 55.9 us  [the longest x1 38.9 us: second_half(): pl.pallas_call(scoped(functools.partial(second_kernel, sizes, scale), tak...]
    unnamed x3 -> x1, local copies, waits for them, and re-layouts: 6.69 us -> 1.3 us
where the time goes in v3:
time: 61.6 us; the launch traced here: 61.3 us
  Pallas kernels  55.9 us (91%)
  between operations  4.1 us (7%)
  local copies, waits for them, and re-layouts  1.3 us (2%)
    pallas_call x1, Pallas kernels, second_half(): pl.pallas_call(scoped(functools.partial(second_kernel, sizes, scale), tak...  38.9 us
    pallas_call x1, Pallas kernels, first_half(): pl.pallas_call(scoped(first_kernel, acc_shapes), out_shape=(jax.ShapeDtyp...  17 us
    unnamed x1, local copies, waits for them, and re-layouts  1.3 us

profile of v3, /device:TPU:1, one launch (start us, length us, event | category | flops | bytes accessed | tf_op | source)
XLA Modules:
  0.0 61.3 jit_solution(4401968260909275651)
XLA Ops:
  0.6 17.0 %shard_map.103 = (f32[2,3,4,4,4,3,128]{6,5,4,3,2,1,0:T(4,128)}, s32[128,128]{1,0:T(8,128)}, s32[128,128]{1,0:T(8,128)}, bf16[32,16,256]{2,1,0:T(8,128)(2,1)}, f32[8,128]{1,0:T(8,128)}) custom-call(s32[32]{0:T(128)} %refs_0_.1, f32[256,128]{1,0:T(8,128)} %bitcast.25, f32[9,256,128]{2,1,0:T(8,128)} %bitcast.21, f32[3,256,128]{2,1,0:T(8,128)} %bitcast.23, ...), custom_call_target="tpu_custom_call" | custom-call | tf_op jit(solution)/shard_map/pallas_call | solution.py:307
  17.6 38.9 %shard_map.104 = (f32[9,128]{1,0:T(8,128)}, f32[1,1]{1,0:T(1,128)}, f32[1,1]{1,0:T(1,128)}) custom-call(f32[256,128]{1,0:T(8,128)} %bitcast.26, f32[9,256,128]{2,1,0:T(8,128)} %bitcast.22, f32[3,256,128]{2,1,0:T(8,128)} %bitcast.24, s32[128,128]{1,0:T(8,128)} %get-tuple-element.11.refs_3_, s32[128,128]{1,0:T(8,128)} %get-tuple-element.12.refs_4_, ...), custom_call_target="tpu_custom_call" | custom-call | tf_op jit(solution)/shard_map/pallas_call | solution.py:538
  56.6 1.3 %copy.17 = f32[9,128]{1,0:T(8,128)} copy(f32[9,128]{1,0:T(8,128)} %get-tuple-element.22) | data formatting | bytes 9216

commit v4 on v3

--- a/solution.py
+++ b/solution.py
@@ -14,6 +14,7 @@
 LANES = 128
 CAM = 9
 BINS = 64
+UNROLL = 4
 
 
 def thirds(value):
@@ -200,12 +201,12 @@
         dots = pltpu.matmul_pop(point_accs[0]) + pltpu.matmul_pop(point_accs[1])
         point_ref[:, pl.ds(base, 2 * LANES)] += (dots[32:48] + dots[16:32]) + dots[0:16]
 
-    def two_tiles(k, _):
-        one_tile(2 * k, 0, 1)
-        one_tile(2 * k + 1, 1, 0)
+    def some_tiles(k, _):
+        for s in range(UNROLL):
+            one_tile(UNROLL * k + s, s % 2, 1 - s % 2)
         return 0
 
-    lax.fori_loop(0, tiles // 2, two_tiles, 0)
+    lax.fori_loop(0, tiles // UNROLL, some_tiles, 0)
     drain(accs, total_ref)
     regroup_into(grad_ref, total_ref)
     point_square = solve_points(point_ref, damp_ref, step_ref)
@@ -269,12 +270,12 @@
         split_lines(ahead, factor, cam_ref, line_ref.at[later])
         move_end(after, pt_ref, res_ref, moved_ref, point_accs)
 
-    def two_tiles(k, _):
-        one_tile(2 * k, 0, 1)
-        one_tile(2 * k + 1, 1, 0)
+    def some_tiles(k, _):
+        for s in range(UNROLL):
+            one_tile(UNROLL * k + s, s % 2, 1 - s % 2)
         return 0
 
-    lax.fori_loop(first // 2, last // 2, two_tiles, 0)
+    lax.fori_loop(first // UNROLL, last // UNROLL, some_tiles, 0)
 
 
 def scoped(kernel, shapes):
@@ -483,36 +484,35 @@
         return jnp.concatenate(own, axis=0)
 
     refs = (index_ref, window_ref, pt_ref, res_ref, moved_ref, pos_ref, cam_ref, line_ref, accs)
+    lane = lax.broadcasted_iota(I32, mine_ref.shape, 1)
     second_start(*refs)
+    second_tiles(0, 8, *refs)
     pl.semaphore_wait(barrier, len(far) + len(near))
     pairs(0, grad_ref)
-    second_tiles(0, 4, *refs)
+    second_tiles(8, 16, *refs)
     phase_one(0, grad_ref)
-    second_tiles(4, 12, *refs)
+    second_tiles(16, 24, *refs)
     phase_two(0)
-    second_tiles(12, 18, *refs)
+    second_tiles(24, 32, *refs)
+    drain(accs[2:], total_ref)
+    regroup_into(move_ref, total_ref)
+    pairs(1, move_ref)
     phase_three(0)
-    second_tiles(18, 24, *refs)
+    phase_one(1, move_ref)
     grads = finish(0)
-    lane = lax.broadcasted_iota(I32, mine_ref.shape, 1)
     mine_ref[...] = sums_ref[...] + jnp.where(lane == 1, jnp.sum(grads * grads), 0.0)
     arrivals = [
         send(mine_ref, far_ref.at[k], far_send.at[k], far_recv.at[k], device)
         for k, device in enumerate(far)
     ]
-    second_tiles(24, 32, *refs)
-    drain(accs[2:], total_ref)
-    regroup_into(move_ref, total_ref)
-    pairs(1, move_ref)
+    phase_two(1)
     for copy in arrivals:
         copy.wait_recv()
     plane_ref[...] = mine_ref[...] + jnp.sum(far_ref[...], axis=0)
-    phase_one(1, move_ref)
     arrivals = [
         send(plane_ref, near_ref.at[k], near_send.at[k], near_recv.at[k], device)
         for k, device in enumerate(near)
     ]
-    phase_two(1)
     phase_three(1)
     for copy in arrivals:
         copy.wait_recv()

time: 61.6 us -> 56.1 us (0.911)
  Pallas kernels: 55.9 us -> 50.5 us
    pallas_call x1, Pallas kernels: 38.9 us -> 34.7 us  [second_half(): pl.pallas_call(scoped(functools.partial(second_kernel, sizes, scale), tak...]
    pallas_call x1, Pallas kernels: 17 us -> 15.8 us  [first_half(): pl.pallas_call(scoped(first_kernel, acc_shapes), out_shape=(jax.ShapeDtyp...]
where the time goes in v4:
time: 56.1 us; the launch traced here: 55.9 us
  Pallas kernels  50.5 us (90%)
  between operations  4.1 us (7%)
  local copies, waits for them, and re-layouts  1.3 us (2%)
    pallas_call x1, Pallas kernels, second_half(): pl.pallas_call(scoped(functools.partial(second_kernel, sizes, scale), tak...  34.7 us
    pallas_call x1, Pallas kernels, first_half(): pl.pallas_call(scoped(first_kernel, acc_shapes), out_shape=(jax.ShapeDtyp...  15.8 us
    unnamed x1, local copies, waits for them, and re-layouts  1.3 us

profile of v4, /device:TPU:1, one launch (start us, length us, event | category | flops | bytes accessed | tf_op | source)
XLA Modules:
  0.0 55.9 jit_solution(8461743962581090466)
XLA Ops:
  0.6 15.8 %shard_map.103 = (f32[2,3,4,4,4,3,128]{6,5,4,3,2,1,0:T(4,128)}, s32[128,128]{1,0:T(8,128)}, s32[128,128]{1,0:T(8,128)}, bf16[32,16,256]{2,1,0:T(8,128)(2,1)}, f32[8,128]{1,0:T(8,128)}) custom-call(s32[32]{0:T(128)} %refs_0_.1, f32[256,128]{1,0:T(8,128)} %bitcast.25, f32[9,256,128]{2,1,0:T(8,128)} %bitcast.21, f32[3,256,128]{2,1,0:T(8,128)} %bitcast.23, ...), custom_call_target="tpu_custom_call" | custom-call | tf_op jit(solution)/shard_map/pallas_call | solution.py:308
  16.4 34.7 %shard_map.104 = (f32[9,128]{1,0:T(8,128)}, f32[1,1]{1,0:T(1,128)}, f32[1,1]{1,0:T(1,128)}) custom-call(f32[256,128]{1,0:T(8,128)} %bitcast.26, f32[9,256,128]{2,1,0:T(8,128)} %bitcast.22, f32[3,256,128]{2,1,0:T(8,128)} %bitcast.24, s32[128,128]{1,0:T(8,128)} %get-tuple-element.11.refs_3_, s32[128,128]{1,0:T(8,128)} %get-tuple-element.12.refs_4_, ...), custom_call_target="tpu_custom_call" | custom-call | tf_op jit(solution)/shard_map/pallas_call | solution.py:538
  51.1 1.3 %copy.17 = f32[9,128]{1,0:T(8,128)} copy(f32[9,128]{1,0:T(8,128)} %get-tuple-element.22) | data formatting | bytes 9216

commit v5 on v4

--- a/solution.py
+++ b/solution.py
@@ -30,10 +30,6 @@
 
 def pair_sum(product):
     return product + pltpu.roll(product, product.shape[0] - 1, 0)
-
-
-def window_base(offset):
-    return pl.multiple_of((offset >> 7) * LANES, LANES)
 
 
 def one_hot(count, index):
@@ -100,11 +96,20 @@
     lax.fori_loop(0, BINS, one, 0, unroll=4)
 
 
+def is_block(offset, count):
+    block = jnp.full((16, LANES), offset >> 7, I32)
+    return [block == b for b in range(count)]
+
+
 def solve_points(point_ref, damp_ref, step_ref):
-    points = damp_ref.shape[0] * LANES
-    damping = row_of(damp_ref, 0, points // LANES)
-    g = [point_ref[k : k + 1, 0:points] for k in range(3)]
-    aa, ab, ac, bb, bc, cc = [point_ref[k : k + 1, 0:points] for k in range(3, 9)]
+    blocks = damp_ref.shape[0]
+    damping = row_of(damp_ref, 0, blocks)
+
+    def row(k):
+        return jnp.concatenate([point_ref[b, k : k + 1, :] for b in range(blocks)], axis=1)
+
+    g = [row(k) for k in range(3)]
+    aa, ab, ac, bb, bc, cc = [row(k) for k in range(3, 9)]
     aa, bb, cc = aa + damping, bb + damping, cc + damping
     cof_aa = bb * cc - bc * bc
     cof_ab = ac * bc - ab * cc
@@ -121,36 +126,32 @@
     step_ref[...] = jnp.zeros_like(step_ref)
     for k in range(3):
         for p, part in enumerate(thirds(steps[k])):
-            step_ref[3 * p + k : 3 * p + k + 1, 0:points] = part.astype(F32)
+            value = part.astype(F32)
+            for b in range(blocks):
+                step_ref[b, 3 * p + k : 3 * p + k + 1, :] = value[:, b * LANES : (b + 1) * LANES]
     return jnp.sum(g[0] * g[0] + g[1] * g[1] + g[2] * g[2])
 
 
-def first_kernel(
+def first_tiles(
     offset_ref,
     res_ref,
     cam_ref,
     pt_ref,
     camera_ref,
     slot_ref,
-    damp_ref,
     table_ref,
-    grad_ref,
     pos_ref,
     index_ref,
-    window_ref,
-    sums_ref,
-    step_ref,
     feat_ref,
     point_ref,
     line_ref,
-    total_ref,
-    *accs,
+    point_accs,
+    accs,
 ):
     tiles = res_ref.shape[0] // 8
-    point_accs, accs = accs[:2], accs[2:]
+    blocks = point_ref.shape[0]
     point_ref[...] = jnp.zeros_like(point_ref)
     feat_ref[...] = jnp.zeros_like(feat_ref)
-    empty_accs(point_accs + accs)
 
     def find(tile):
         lines = pl.ds(pl.multiple_of(tile * 4, 4), 4)
@@ -178,14 +179,14 @@
         offset = offset_ref[tile]
         lines = pl.ds(pl.multiple_of(tile * 4, 4), 4)
         index_ref[lines, :] = slot_ref[lines, :] + (offset & 127)
-        index, base = row_of(index_ref, tile * 4, 4), window_base(offset)
+        index = row_of(index_ref, tile * 4, 4)
         for unit in range(2):
             columns = [feat_ref[pl.ds(4 * unit + 2 * q, 16, stride=8), :] for q in range(2)]
             lhs = jnp.concatenate(thirds(jnp.concatenate(columns, axis=1)), axis=0)
             hot = one_hot(2 * LANES, index[:, unit * 2 * LANES : (unit + 1) * 2 * LANES])
             pltpu.matmul_push_rhs(hot, 1, unit, transpose=True)
             pltpu.matmul_acc_lhs(point_accs[unit], lhs, 1)
-        return base
+        return is_block(offset, blocks - 1)
 
     find(0)
     push_bins(0, pos_ref)
@@ -194,12 +195,16 @@
     def one_tile(tile, now, later):
         ahead = jnp.minimum(tile + 1, tiles - 1)
         add_lines(tile, pos_ref, line_ref.at[now], accs)
-        base = add_points(tile)
+        here = add_points(tile)
         find(ahead)
         push_bins(ahead, pos_ref)
         split_lines(ahead, residual_of(ahead), cam_ref, line_ref.at[later])
         dots = pltpu.matmul_pop(point_accs[0]) + pltpu.matmul_pop(point_accs[1])
-        point_ref[:, pl.ds(base, 2 * LANES)] += (dots[32:48] + dots[16:32]) + dots[0:16]
+        dots = (dots[32:48] + dots[16:32]) + dots[0:16]
+        left, right = dots[:, :LANES], dots[:, LANES:]
+        for b in range(blocks):
+            part = jnp.where(here[b - 1], right, 0.0) if b else jnp.zeros_like(left)
+            point_ref[b] += jnp.where(here[b], left, part) if b < blocks - 1 else part
 
     def some_tiles(k, _):
         for s in range(UNROLL):
@@ -207,24 +212,17 @@
         return 0
 
     lax.fori_loop(0, tiles // UNROLL, some_tiles, 0)
-    drain(accs, total_ref)
-    regroup_into(grad_ref, total_ref)
-    point_square = solve_points(point_ref, damp_ref, step_ref)
-
-    def cut_window(tile, _):
-        window_ref[tile] = step_ref[:, pl.ds(window_base(offset_ref[tile]), 2 * LANES)].astype(BF16)
-        return 0
-
-    lax.fori_loop(0, tiles, cut_window, 0, unroll=4)
-    residual = res_ref[...]
-    cost = jnp.sum(residual * residual)
-    lane = lax.broadcasted_iota(I32, sums_ref.shape, 1)
-    sums_ref[...] = jnp.where(lane == 0, cost, jnp.where(lane == 1, point_square, 0.0))
-
-
-def move_start(tile, index_ref, window_ref, point_accs):
+
+
+def move_start(tile, offset_ref, index_ref, step_ref, point_accs):
     index = row_of(index_ref, tile * 4, 4)
-    lhs = window_ref[tile]
+    blocks = step_ref.shape[0]
+    here = is_block(offset_ref[tile], blocks - 1)
+    left = right = jnp.zeros((16, LANES), F32)
+    for b in range(blocks - 1):
+        left = jnp.where(here[b], step_ref[b], left)
+        right = jnp.where(here[b], step_ref[b + 1], right)
+    lhs = jnp.concatenate([left, right], axis=1).astype(BF16)
     for unit in range(2):
         hot = one_hot(2 * LANES, index[:, unit * 2 * LANES : (unit + 1) * 2 * LANES])
         pltpu.matmul_push_rhs(hot, 1, unit)
@@ -244,27 +242,24 @@
                 moved_ref[pl.ds(row, 1), :] = moved - res_ref[pl.ds(row, 1), :]
 
 
-def second_start(index_ref, window_ref, pt_ref, res_ref, moved_ref, pos_ref, cam_ref, line_ref, accs):
-    point_accs, accs = accs[:2], accs[2:]
-    empty_accs(point_accs + accs)
+def second_start(offset_ref, index_ref, step_ref, pt_ref, res_ref, moved_ref, pos_ref, cam_ref, line_ref, point_accs, accs):
     for tile in range(2):
-        move_start(tile, index_ref, window_ref, point_accs)
+        move_start(tile, offset_ref, index_ref, step_ref, point_accs)
         move_end(tile, pt_ref, res_ref, moved_ref, point_accs)
     push_bins(0, pos_ref)
     split_lines(0, moved_ref[0:8, :], cam_ref, line_ref.at[0])
 
 
 def second_tiles(
-    first, last, index_ref, window_ref, pt_ref, res_ref, moved_ref, pos_ref, cam_ref, line_ref, accs
+    first, last, offset_ref, index_ref, step_ref, pt_ref, res_ref, moved_ref, pos_ref, cam_ref, line_ref, point_accs, accs
 ):
     tiles = res_ref.shape[0] // 8
-    point_accs, accs = accs[:2], accs[2:]
 
     def one_tile(tile, now, later):
         ahead = jnp.minimum(tile + 1, tiles - 1)
         after = jnp.minimum(tile + 2, tiles - 1)
         add_lines(tile, pos_ref, line_ref.at[now], accs)
-        move_start(after, index_ref, window_ref, point_accs)
+        move_start(after, offset_ref, index_ref, step_ref, point_accs)
         push_bins(ahead, pos_ref)
         factor = moved_ref[pl.ds(pl.multiple_of(ahead * 8, 8), 8), :]
         split_lines(ahead, factor, cam_ref, line_ref.at[later])
@@ -286,13 +281,9 @@
 
 
 def acc_shapes():
-    points = [pltpu.ACC(unit)((48, 2 * LANES), F32) for unit in range(2)]
-    return points + [pltpu.ACC(unit)((BINS, 2 * LANES), F32) for unit in range(2) for _ in range(CAM)]
-
-
-def take_shapes():
-    points = [pltpu.ACC(unit)((16, 2 * LANES), F32) for unit in range(2)]
-    return points + acc_shapes()[2:]
+    sums = [pltpu.ACC(unit)((48, 2 * LANES), F32) for unit in range(2)]
+    takes = [pltpu.ACC(unit)((16, 2 * LANES), F32) for unit in range(2)]
+    return sums + takes + [pltpu.ACC(unit)((BINS, 2 * LANES), F32) for unit in range(2) for _ in range(CAM)]
 
 
 def row_major(array):
@@ -300,30 +291,6 @@
     blocks = array.reshape(2, *rows, n_obs // LANES, LANES)
     blocks = jnp.moveaxis(blocks, 0, -2)
     return blocks.reshape(*rows, 2 * n_obs // LANES, LANES)
-
-
-def first_half(residual, cam_jacobian, point_jacobian, obs_camera, obs_slot, tile_offset, damping, camera_slot):
-    vmem = pl.BlockSpec(memory_space=pltpu.VMEM)
-    points = damping.shape[0]
-    return pl.pallas_call(
-        scoped(first_kernel, acc_shapes),
-        out_shape=(
-            jax.ShapeDtypeStruct((2, 3, 4, 4, 4, 3, LANES), F32),
-            jax.ShapeDtypeStruct(obs_camera.shape, I32),
-            jax.ShapeDtypeStruct(obs_camera.shape, I32),
-            jax.ShapeDtypeStruct((tile_offset.size, 16, 2 * LANES), BF16),
-            jax.ShapeDtypeStruct((8, LANES), F32),
-        ),
-        in_specs=[pl.BlockSpec(memory_space=pltpu.SMEM)] + [vmem] * 7,
-        out_specs=(vmem,) * 5,
-        scratch_shapes=[
-            pltpu.VMEM((16, damping.size + LANES), F32),
-            pltpu.VMEM((16 * 8, LANES), F32),
-            pltpu.VMEM((16, damping.size + LANES), F32),
-            pltpu.VMEM((2, 2, CAM, 8, LANES), F32),
-            pltpu.VMEM((2, CAM * BINS, LANES), F32),
-        ],
-    )(tile_offset, residual, cam_jacobian, point_jacobian, obs_camera, obs_slot, damping, camera_slot)
 
 
 AXES = ("gx_0", "gx_1", "gy_0", "gy_1")
@@ -354,23 +321,29 @@
     return (slice(None),) * position + (index,)
 
 
-def second_kernel(
+def whole_kernel(
     sizes,
     scale,
+    offset_ref,
     res_ref,
     cam_ref,
     pt_ref,
-    pos_ref,
-    index_ref,
-    window_ref,
-    grad_ref,
-    sums_ref,
+    camera_ref,
+    slot_ref,
+    damp_ref,
+    table_ref,
     reduced_ref,
     cost_ref,
     norm_ref,
+    pos_ref,
+    index_ref,
+    feat_ref,
+    point_ref,
+    step_ref,
     moved_ref,
     line_ref,
     total_ref,
+    grad_ref,
     move_ref,
     pair_ref,
     whole_ref,
@@ -483,24 +456,60 @@
         own = [gather(sum2_ref, in3_ref, flight[job][g], job, g, 2, 0) for g in range(3)]
         return jnp.concatenate(own, axis=0)
 
-    refs = (index_ref, window_ref, pt_ref, res_ref, moved_ref, pos_ref, cam_ref, line_ref, accs)
+    sum_accs, take_accs, accs = accs[:2], accs[2:4], accs[4:]
+    empty_accs(sum_accs + take_accs + accs)
+    first_tiles(
+        offset_ref,
+        res_ref,
+        cam_ref,
+        pt_ref,
+        camera_ref,
+        slot_ref,
+        table_ref,
+        pos_ref,
+        index_ref,
+        feat_ref,
+        point_ref,
+        line_ref,
+        sum_accs,
+        accs,
+    )
+    drain(accs, total_ref)
+    regroup_into(grad_ref, total_ref)
+    pl.semaphore_wait(barrier, len(far) + len(near))
+    pairs(0, grad_ref)
+    point_square = solve_points(point_ref, damp_ref, step_ref)
+    residual = res_ref[...]
+    square = jnp.sum(residual * residual)
     lane = lax.broadcasted_iota(I32, mine_ref.shape, 1)
+    refs = (
+        offset_ref,
+        index_ref,
+        step_ref,
+        pt_ref,
+        res_ref,
+        moved_ref,
+        pos_ref,
+        cam_ref,
+        line_ref,
+        take_accs,
+        accs,
+    )
     second_start(*refs)
     second_tiles(0, 8, *refs)
-    pl.semaphore_wait(barrier, len(far) + len(near))
-    pairs(0, grad_ref)
+    phase_one(0, grad_ref)
     second_tiles(8, 16, *refs)
-    phase_one(0, grad_ref)
+    phase_two(0)
     second_tiles(16, 24, *refs)
-    phase_two(0)
+    phase_three(0)
     second_tiles(24, 32, *refs)
-    drain(accs[2:], total_ref)
+    drain(accs, total_ref)
     regroup_into(move_ref, total_ref)
     pairs(1, move_ref)
-    phase_three(0)
     phase_one(1, move_ref)
     grads = finish(0)
-    mine_ref[...] = sums_ref[...] + jnp.where(lane == 1, jnp.sum(grads * grads), 0.0)
+    gradient_square = point_square + jnp.sum(grads * grads)
+    mine_ref[...] = jnp.where(lane == 0, square, jnp.where(lane == 1, gradient_square, 0.0))
     arrivals = [
         send(mine_ref, far_ref.at[k], far_send.at[k], far_recv.at[k], device)
         for k, device in enumerate(far)
@@ -527,7 +536,9 @@
         copy.wait_send()
 
 
-def second_half(residual, cam_jacobian, point_jacobian, pos, index, window, grad, sums, sizes, scale):
+def whole(
+    residual, cam_jacobian, point_jacobian, obs_camera, obs_slot, tile_offset, damping, camera_slot, sizes, scale
+):
     vmem = pl.BlockSpec(memory_space=pltpu.VMEM)
     smem = pl.BlockSpec(memory_space=pltpu.SMEM)
     rows = CAM // 3
@@ -536,18 +547,24 @@
     far = sizes["gx_0"] * sizes["gx_1"] - 1
     near = sizes["gy_0"] * sizes["gy_1"] - 1
     return pl.pallas_call(
-        scoped(functools.partial(second_kernel, sizes, scale), take_shapes),
+        scoped(functools.partial(whole_kernel, sizes, scale), acc_shapes),
         out_shape=(
             jax.ShapeDtypeStruct((CAM, LANES), F32),
             jax.ShapeDtypeStruct((1, 1), F32),
             jax.ShapeDtypeStruct((1, 1), F32),
         ),
-        in_specs=[vmem] * 8,
+        in_specs=[smem] + [vmem] * 7,
         out_specs=(vmem, smem, smem),
         scratch_shapes=[
+            pltpu.VMEM(obs_camera.shape, I32),
+            pltpu.VMEM(obs_camera.shape, I32),
+            pltpu.VMEM((16 * 8, LANES), F32),
+            pltpu.VMEM((damping.shape[0] + 1, 16, LANES), F32),
+            pltpu.VMEM((damping.shape[0] + 1, 16, LANES), F32),
             pltpu.VMEM(residual.shape, F32),
             pltpu.VMEM((2, 2, CAM, 8, LANES), F32),
             pltpu.VMEM((2, CAM * BINS, LANES), F32),
+            buffer(2, 3, 4, 4, 4),
             buffer(2, 3, 4, 4, 4),
             buffer(2, 3, 4, 4, 4),
             buffer(2, 3, 4, 4, 4),
@@ -570,7 +587,7 @@
             dma((near,)),
         ],
         compiler_params=pltpu.CompilerParams(collective_id=0, has_side_effects=True),
-    )(residual, cam_jacobian, point_jacobian, pos, index, window, grad, sums)
+    )(tile_offset, residual, cam_jacobian, point_jacobian, obs_camera, obs_slot, damping, camera_slot)
 
 
 def on_device(
@@ -582,10 +599,9 @@
     scale = (2.0 * n_obs * devices, 9.0 * camera_slot.shape[0] + 3.0 * damping.shape[0] * devices)
     lines = lambda array: array.reshape(-1, LANES)
     res, cam, pt = row_major(residual), row_major(cam_jacobian), row_major(point_jacobian)
-    grad, pos, index, window, sums = first_half(
-        res, cam, pt, lines(obs_camera), lines(obs_slot), tile_offset, lines(damping), lines(camera_slot)
+    reduced, cost, norm = whole(
+        res, cam, pt, lines(obs_camera), lines(obs_slot), tile_offset, lines(damping), lines(camera_slot), sizes, scale
     )
-    reduced, cost, norm = second_half(res, cam, pt, pos, index, window, grad, sums, sizes, scale)
     return (reduced, cost.reshape(()), norm.reshape(()))
 
 

time: 56.1 us -> 54 us (0.963)
  Pallas kernels: 50.5 us -> 48.3 us
    pallas_call x2 -> x1, Pallas kernels: 50.5 us -> 48.3 us  [whole(): pl.pallas_call(scoped(functools.partial(whole_kernel, sizes, scale), acc_...]
where the time goes in v5:
time: 54 us; the launch traced here: 53.7 us
  Pallas kernels  48.3 us (89%)
  between operations  4.16 us (8%)
  local copies, waits for them, and re-layouts  1.3 us (2%)
    pallas_call x1, Pallas kernels, whole(): pl.pallas_call(scoped(functools.partial(whole_kernel, sizes, scale), acc_...  48.3 us
    unnamed x1, local copies, waits for them, and re-layouts  1.3 us

profile of v5, /device:TPU:1, one launch (start us, length us, event | category | flops | bytes accessed | tf_op | source)
XLA Modules:
  0.0 53.7 jit_solution(7695442534980472236)
XLA Ops:
  0.6 48.3 %shard_map.103 = (f32[9,128]{1,0:T(8,128)}, f32[1,1]{1,0:T(1,128)}, f32[1,1]{1,0:T(1,128)}) custom-call(s32[32]{0:T(128)} %refs_0_.1, f32[256,128]{1,0:T(8,128)} %bitcast.23, f32[9,256,128]{2,1,0:T(8,128)} %bitcast.21, f32[3,256,128]{2,1,0:T(8,128)} %bitcast.22, s32[128,128]{1,0:T(8,128)} %bitcast.24, s32[128,128]{1,0:T(8,128)} %bitcast.25, ...), custom_call_target="tpu_custom_call" | custom-call | tf_op jit(solution)/shard_map/pallas_call | solution.py:549
  48.9 1.3 %copy.17 = f32[9,128]{1,0:T(8,128)} copy(f32[9,128]{1,0:T(8,128)} %get-tuple-element.12) | data formatting | bytes 9216

commit v6 on v5

--- a/solution.py
+++ b/solution.py
@@ -14,7 +14,8 @@
 LANES = 128
 CAM = 9
 BINS = 64
-UNROLL = 4
+PITCH = 72
+UNROLL = 8
 
 
 def thirds(value):
@@ -81,16 +82,15 @@
         pltpu.matmul_acc_lhs(accs[unit * CAM], jnp.zeros((BINS, 2 * LANES), BF16), 0)
     for m in range(CAM):
         total = pltpu.matmul_pop(accs[m]) + pltpu.matmul_pop(accs[CAM + m])
-        total_ref[0, m * BINS : (m + 1) * BINS] = total[:, :LANES]
-        total_ref[1, m * BINS : (m + 1) * BINS] = total[:, LANES:]
+        total_ref[0, m * PITCH : m * PITCH + BINS] = total[:, :LANES]
+        total_ref[1, m * PITCH : m * PITCH + BINS] = total[:, LANES:]
 
 
 def regroup_into(out_ref, total_ref):
     def one(hi, _):
         for side in range(2):
-            for g in range(3):
-                rows = pl.ds(g * 3 * BINS + hi, 3, stride=BINS)
-                out_ref[side, g, hi >> 4, (hi >> 2) & 3, hi & 3] = total_ref[side, rows, :]
+            rows = pl.ds(hi, CAM, stride=PITCH)
+            out_ref[side, hi >> 4, (hi >> 2) & 3, hi & 3] = total_ref[side, rows, :]
         return 0
 
     lax.fori_loop(0, BINS, one, 0, unroll=4)
@@ -294,9 +294,8 @@
 
 
 AXES = ("gx_0", "gx_1", "gy_0", "gy_1")
-RINGS = ("gx_0", "gy_0", "gy_1")
-ORDERS = ((0, 1, 2), (1, 2, 0), (2, 0, 1))
-SPOTS = (0, 1, 0)
+HOPS = (0, 1, 2, 1)
+SLABS = (2, 1, 3, 0)
 
 
 def neighbours(me, names, sizes):
@@ -317,8 +316,9 @@
     return found
 
 
-def inside(position, index):
-    return (slice(None),) * position + (index,)
+def slab_offsets(dx):
+    found = [(dx, dy, dz) for dy in range(4) for dz in range(4) if (dx, dy, dz) != (0, 0, 0)]
+    return sorted(found, key=lambda offset: -sum(HOPS[d] for d in offset))
 
 
 def whole_kernel(
@@ -332,7 +332,8 @@
     slot_ref,
     damp_ref,
     table_ref,
-    reduced_ref,
+    kept_ref,
+    rest_ref,
     cost_ref,
     norm_ref,
     pos_ref,
@@ -347,19 +348,15 @@
     move_ref,
     pair_ref,
     whole_ref,
-    in1_ref,
-    sum1_ref,
-    in2_ref,
-    sum2_ref,
-    in3_ref,
+    inbox_ref,
     mine_ref,
     far_ref,
     plane_ref,
     near_ref,
     pair_send,
     pair_recv,
-    ring_send,
-    ring_recv,
+    chip_send,
+    chip_recv,
     far_send,
     far_recv,
     near_send,
@@ -369,12 +366,17 @@
     me = {name: lax.axis_index(name) for name in AXES}
     far = neighbours(me, ("gx_0", "gx_1"), sizes)
     near = neighbours(me, ("gy_0", "gy_1"), sizes)
-    rings = [neighbours(me, (name,), sizes) for name in RINGS]
     core = me["gx_1"]
     partner = (me["gx_0"], 1 - core, me["gy_0"], me["gy_1"])
 
     barrier = pltpu.get_barrier_semaphore()
-    for target in far + near:
+    chips = {}
+    for dx in SLABS:
+        for offset in slab_offsets(dx):
+            place = [lax.rem(me[n] + d, sizes[n]) for n, d in zip(("gx_0", "gy_0", "gy_1"), offset)]
+            chips[offset] = (place[0], core, place[1], place[2])
+    others = [chips[o] for o in chips if o[0] and (o[1] or o[2])]
+    for target in far + near + others:
         pl.semaphore_signal(barrier, inc=1, device_id=target, device_id_type=MESH)
 
     started = []
@@ -392,69 +394,47 @@
         started.append(copy)
         return copy
 
-    def spread(source, inbox, job, group, phase, position):
-        ring = ORDERS[group][phase]
-        name = RINGS[ring]
-        copies = []
-        for k, device in enumerate(rings[ring]):
-            there = device[AXES.index(name)]
-            copies.append(
+    flight = {}
+
+    def pairs(job, source):
+        flight[job] = []
+        for k, dx in enumerate(SLABS):
+            there = lax.rem(me["gx_0"] + dx, sizes["gx_0"])
+            flight[job].append(
                 send(
-                    source.at[(job, group) + inside(position, there)],
-                    inbox.at[job, group, k],
-                    ring_send.at[job, group, phase, k],
-                    ring_recv.at[job, group, phase, k],
-                    device,
+                    source.at[1 - core, there],
+                    pair_ref.at[job, there],
+                    pair_send.at[job, k],
+                    pair_recv.at[job, k],
+                    partner,
                 )
             )
-        return copies
-
-    def gather(source, inbox, copies, job, group, phase, position):
-        for copy in copies:
-            copy.wait_recv()
-        here = me[RINGS[ORDERS[group][phase]]]
-        kept = source[(job, group) + inside(position, here)]
-        return (kept + inbox[job, group, 1]) + (inbox[job, group, 0] + inbox[job, group, 2])
-
-    flight = {}
-
-    def pairs(job, source):
-        flight[job] = [
-            send(
-                source.at[1 - core, g],
-                pair_ref.at[job, g],
-                pair_send.at[job, g],
-                pair_recv.at[job, g],
-                partner,
-            )
-            for g in range(3)
-        ]
-
-    def phase_one(job, source):
+
+    def spread(job, source):
         copies = flight[job]
         flight[job] = []
-        for g in range(3):
-            copies[g].wait_recv()
-            whole_ref[job, g] = source[core, g] + pair_ref[job, g]
-            flight[job].append(spread(whole_ref, in1_ref, job, g, 0, ORDERS[g][0]))
-
-    def phase_two(job):
-        copies = flight[job]
-        flight[job] = []
-        for g in range(3):
-            sum1_ref[job, g] = gather(whole_ref, in1_ref, copies[g], job, g, 0, ORDERS[g][0])
-            flight[job].append(spread(sum1_ref, in2_ref, job, g, 1, SPOTS[g]))
-
-    def phase_three(job):
-        copies = flight[job]
-        flight[job] = []
-        for g in range(3):
-            sum2_ref[job, g] = gather(sum1_ref, in2_ref, copies[g], job, g, 1, SPOTS[g])
-            flight[job].append(spread(sum2_ref, in3_ref, job, g, 2, 0))
+        for k, dx in enumerate(SLABS):
+            there = lax.rem(me["gx_0"] + dx, sizes["gx_0"])
+            copies[k].wait_recv()
+            whole_ref[job, there] = source[core, there] + pair_ref[job, there]
+            for offset in slab_offsets(dx):
+                slot = (offset[0] * 4 + offset[1]) * 4 + offset[2] - 1
+                device = chips[offset]
+                flight[job].append(
+                    send(
+                        whole_ref.at[job, there, device[2], device[3]],
+                        inbox_ref.at[job, slot],
+                        chip_send.at[job, slot],
+                        chip_recv.at[job, slot],
+                        device,
+                    )
+                )
 
     def finish(job):
-        own = [gather(sum2_ref, in3_ref, flight[job][g], job, g, 2, 0) for g in range(3)]
-        return jnp.concatenate(own, axis=0)
+        for copy in flight[job]:
+            copy.wait_recv()
+        kept = whole_ref[job, me["gx_0"], me["gy_0"], me["gy_1"]]
+        return kept, jnp.sum(inbox_ref[job], axis=0)
 
     sum_accs, take_accs, accs = accs[:2], accs[2:4], accs[4:]
     empty_accs(sum_accs + take_accs + accs)
@@ -476,7 +456,7 @@
     )
     drain(accs, total_ref)
     regroup_into(grad_ref, total_ref)
-    pl.semaphore_wait(barrier, len(far) + len(near))
+    pl.semaphore_wait(barrier, len(far) + len(near) + len(others))
     pairs(0, grad_ref)
     point_square = solve_points(point_ref, damp_ref, step_ref)
     residual = res_ref[...]
@@ -497,24 +477,20 @@
     )
     second_start(*refs)
     second_tiles(0, 8, *refs)
-    phase_one(0, grad_ref)
-    second_tiles(8, 16, *refs)
-    phase_two(0)
-    second_tiles(16, 24, *refs)
-    phase_three(0)
-    second_tiles(24, 32, *refs)
-    drain(accs, total_ref)
-    regroup_into(move_ref, total_ref)
-    pairs(1, move_ref)
-    phase_one(1, move_ref)
-    grads = finish(0)
+    spread(0, grad_ref)
+    second_tiles(8, 24, *refs)
+    kept, rest = finish(0)
+    grads = kept + rest
     gradient_square = point_square + jnp.sum(grads * grads)
     mine_ref[...] = jnp.where(lane == 0, square, jnp.where(lane == 1, gradient_square, 0.0))
     arrivals = [
         send(mine_ref, far_ref.at[k], far_send.at[k], far_recv.at[k], device)
         for k, device in enumerate(far)
     ]
-    phase_two(1)
+    second_tiles(24, 32, *refs)
+    drain(accs, total_ref)
+    regroup_into(move_ref, total_ref)
+    pairs(1, move_ref)
     for copy in arrivals:
         copy.wait_recv()
     plane_ref[...] = mine_ref[...] + jnp.sum(far_ref[...], axis=0)
@@ -522,7 +498,7 @@
         send(plane_ref, near_ref.at[k], near_send.at[k], near_recv.at[k], device)
         for k, device in enumerate(near)
     ]
-    phase_three(1)
+    spread(1, move_ref)
     for copy in arrivals:
         copy.wait_recv()
     totals = plane_ref[...] + jnp.sum(near_ref[...], axis=0)
@@ -531,7 +507,7 @@
     norm = jnp.sqrt(totals / scale[1] + 1e-06)
     cost_ref[0, 0] = jnp.sum(jnp.where(first_row & (lane == 0), cost, 0.0))
     norm_ref[0, 0] = jnp.sum(jnp.where(first_row & (lane == 1), norm, 0.0))
-    reduced_ref[...] = finish(1)
+    kept_ref[...], rest_ref[...] = finish(1)
     for copy in started:
         copy.wait_send()
 
@@ -541,8 +517,8 @@
 ):
     vmem = pl.BlockSpec(memory_space=pltpu.VMEM)
     smem = pl.BlockSpec(memory_space=pltpu.SMEM)
-    rows = CAM // 3
-    buffer = lambda *lead: pltpu.VMEM(lead + (rows, LANES), F32)
+    buffer = lambda *lead: pltpu.VMEM(lead + (CAM, LANES), F32)
+    chips = sizes["gx_0"] * sizes["gy_0"] * sizes["gy_1"] - 1
     dma = pltpu.SemaphoreType.DMA
     far = sizes["gx_0"] * sizes["gx_1"] - 1
     near = sizes["gy_0"] * sizes["gy_1"] - 1
@@ -550,11 +526,12 @@
         scoped(functools.partial(whole_kernel, sizes, scale), acc_shapes),
         out_shape=(
             jax.ShapeDtypeStruct((CAM, LANES), F32),
+            jax.ShapeDtypeStruct((CAM, LANES), F32),
             jax.ShapeDtypeStruct((1, 1), F32),
             jax.ShapeDtypeStruct((1, 1), F32),
         ),
         in_specs=[smem] + [vmem] * 7,
-        out_specs=(vmem, smem, smem),
+        out_specs=(vmem, vmem, smem, smem),
         scratch_shapes=[
             pltpu.VMEM(obs_camera.shape, I32),
             pltpu.VMEM(obs_camera.shape, I32),
@@ -563,24 +540,20 @@
             pltpu.VMEM((damping.shape[0] + 1, 16, LANES), F32),
             pltpu.VMEM(residual.shape, F32),
             pltpu.VMEM((2, 2, CAM, 8, LANES), F32),
-            pltpu.VMEM((2, CAM * BINS, LANES), F32),
-            buffer(2, 3, 4, 4, 4),
-            buffer(2, 3, 4, 4, 4),
-            buffer(2, 3, 4, 4, 4),
-            buffer(2, 3, 4, 4, 4),
-            buffer(2, 3, 3, 4, 4),
-            buffer(2, 3, 4, 4),
-            buffer(2, 3, 3, 4),
-            buffer(2, 3, 4),
-            buffer(2, 3, 3),
+            pltpu.VMEM((2, CAM * PITCH, LANES), F32),
+            buffer(2, 4, 4, 4),
+            buffer(2, 4, 4, 4),
+            buffer(2, 4, 4, 4),
+            buffer(2, 4, 4, 4),
+            buffer(2, chips),
             pltpu.VMEM((8, LANES), F32),
             pltpu.VMEM((far, 8, LANES), F32),
             pltpu.VMEM((8, LANES), F32),
             pltpu.VMEM((near, 8, LANES), F32),
-            dma((2, 3)),
-            dma((2, 3)),
-            dma((2, 3, 3, 3)),
-            dma((2, 3, 3, 3)),
+            dma((2, 4)),
+            dma((2, 4)),
+            dma((2, chips)),
+            dma((2, chips)),
             dma((far,)),
             dma((far,)),
             dma((near,)),
@@ -599,10 +572,10 @@
     scale = (2.0 * n_obs * devices, 9.0 * camera_slot.shape[0] + 3.0 * damping.shape[0] * devices)
     lines = lambda array: array.reshape(-1, LANES)
     res, cam, pt = row_major(residual), row_major(cam_jacobian), row_major(point_jacobian)
-    reduced, cost, norm = whole(
+    kept, rest, cost, norm = whole(
         res, cam, pt, lines(obs_camera), lines(obs_slot), tile_offset, lines(damping), lines(camera_slot), sizes, scale
     )
-    return (reduced, cost.reshape(()), norm.reshape(()))
+    return (kept + rest, cost.reshape(()), norm.reshape(()))
 
 
 def solution(mesh):

time: 54 us -> 50.9 us (0.943)
  Pallas kernels: 48.3 us -> 45.2 us
  other arithmetic: 0 us -> 1.32 us
  local copies, waits for them, and re-layouts: 1.3 us -> 0 us
    pallas_call x1, Pallas kernels: 48.3 us -> 45.2 us  [whole(): pl.pallas_call(scoped(functools.partial(whole_kernel, sizes, scale), acc_...]
    add x0 -> x1, other arithmetic: none -> 1.32 us  [on_device(): return (kept + rest, cost.reshape(()), norm.reshape(()))]
    unnamed x1 -> x0, local copies, waits for them, and re-layouts: 1.3 us -> none
where the time goes in v6:
time: 50.9 us; the launch traced here: 50.6 us
  Pallas kernels  45.2 us (89%)
  between operations  4.14 us (8%)
  other arithmetic  1.32 us (3%)
    pallas_call x1, Pallas kernels, whole(): pl.pallas_call(scoped(functools.partial(whole_kernel, sizes, scale), acc_...  45.2 us
    add x1, other arithmetic, on_device(): return (kept + rest, cost.reshape(()), norm.reshape(()))  1.32 us

profile of v6, /device:TPU:1, one launch (start us, length us, event | category | flops | bytes accessed | tf_op | source)
XLA Modules:
  0.0 50.6 jit_solution(8623111827817173240)
XLA Ops:
  0.6 45.2 %shard_map.103 = (f32[9,128]{1,0:T(8,128)}, f32[9,128]{1,0:T(8,128)}, f32[1,1]{1,0:T(1,128)}, f32[1,1]{1,0:T(1,128)}) custom-call(s32[32]{0:T(128)} %refs_0_.1, f32[256,128]{1,0:T(8,128)} %bitcast.23, f32[9,256,128]{2,1,0:T(8,128)} %bitcast.21, f32[3,256,128]{2,1,0:T(8,128)} %bitcast.22, s32[128,128]{1,0:T(8,128)} %bitcast.24, s32[128,128]{1,0:T(8,128)} %bitcast.25, ...), custom_call_target="tpu_custom_call" | custom-call | tf_op jit(solution)/shard_map/pallas_call | solution.py:525
  45.8 1.3 %add.3 = f32[9,128]{1,0:T(8,128)} add(f32[9,128]{1,0:T(8,128)} %get-tuple-element.7, f32[9,128]{1,0:T(8,128)} %get-tuple-element.8) | non-fusion elementwise | flops 1152 | bytes 13824 | tf_op jit(solution)/shard_map/add | solution.py:578

commit v7 on v6

--- a/solution.py
+++ b/solution.py
@@ -147,6 +147,7 @@
     line_ref,
     point_accs,
     accs,
+    loads,
 ):
     tiles = res_ref.shape[0] // 8
     blocks = point_ref.shape[0]
@@ -188,7 +189,11 @@
             pltpu.matmul_acc_lhs(point_accs[unit], lhs, 1)
         return is_block(offset, blocks - 1)
 
+    for load in loads[:2]:
+        load.wait()
     find(0)
+    for load in loads[2:]:
+        load.wait()
     push_bins(0, pos_ref)
     split_lines(0, residual_of(0), cam_ref, line_ref.at[0])
 
@@ -325,6 +330,16 @@
     sizes,
     scale,
     offset_ref,
+    res_hbm,
+    cam_hbm,
+    pt_hbm,
+    camera_hbm,
+    slot_hbm,
+    damp_hbm,
+    table_hbm,
+    kept_ref,
+    rest_ref,
+    cost_ref,
     res_ref,
     cam_ref,
     pt_ref,
@@ -332,10 +347,7 @@
     slot_ref,
     damp_ref,
     table_ref,
-    kept_ref,
-    rest_ref,
-    cost_ref,
-    norm_ref,
+    load_sem,
     pos_ref,
     index_ref,
     feat_ref,
@@ -363,6 +375,22 @@
     near_recv,
     *accs,
 ):
+    loads = [
+        pltpu.make_async_copy(source, target, load_sem.at[k])
+        for k, (source, target) in enumerate(
+            (
+                (camera_hbm, camera_ref),
+                (table_hbm, table_ref),
+                (res_hbm, res_ref),
+                (pt_hbm, pt_ref),
+                (slot_hbm, slot_ref),
+                (cam_hbm, cam_ref),
+                (damp_hbm, damp_ref),
+            )
+        )
+    ]
+    for load in loads:
+        load.start()
     me = {name: lax.axis_index(name) for name in AXES}
     far = neighbours(me, ("gx_0", "gx_1"), sizes)
     near = neighbours(me, ("gy_0", "gy_1"), sizes)
@@ -453,6 +481,7 @@
         line_ref,
         sum_accs,
         accs,
+        loads,
     )
     drain(accs, total_ref)
     regroup_into(grad_ref, total_ref)
@@ -505,8 +534,7 @@
     first_row = lax.broadcasted_iota(I32, mine_ref.shape, 0) == 0
     cost = totals / scale[0]
     norm = jnp.sqrt(totals / scale[1] + 1e-06)
-    cost_ref[0, 0] = jnp.sum(jnp.where(first_row & (lane == 0), cost, 0.0))
-    norm_ref[0, 0] = jnp.sum(jnp.where(first_row & (lane == 1), norm, 0.0))
+    cost_ref[...] = jnp.where(lane == 0, cost, norm)
     kept_ref[...], rest_ref[...] = finish(1)
     for copy in started:
         copy.wait_send()
@@ -527,12 +555,19 @@
         out_shape=(
             jax.ShapeDtypeStruct((CAM, LANES), F32),
             jax.ShapeDtypeStruct((CAM, LANES), F32),
-            jax.ShapeDtypeStruct((1, 1), F32),
-            jax.ShapeDtypeStruct((1, 1), F32),
+            jax.ShapeDtypeStruct((8, LANES), F32),
         ),
-        in_specs=[smem] + [vmem] * 7,
-        out_specs=(vmem, vmem, smem, smem),
+        in_specs=[smem] + [pl.BlockSpec(memory_space=pl.ANY)] * 7,
+        out_specs=(vmem, vmem, vmem),
         scratch_shapes=[
+            pltpu.VMEM(residual.shape, F32),
+            pltpu.VMEM(cam_jacobian.shape, F32),
+            pltpu.VMEM(point_jacobian.shape, F32),
+            pltpu.VMEM(obs_camera.shape, I32),
+            pltpu.VMEM(obs_slot.shape, I32),
+            pltpu.VMEM(damping.shape, F32),
+            pltpu.VMEM(camera_slot.shape, I32),
+            dma((7,)),
             pltpu.VMEM(obs_camera.shape, I32),
             pltpu.VMEM(obs_camera.shape, I32),
             pltpu.VMEM((16 * 8, LANES), F32),
@@ -572,10 +607,10 @@
     scale = (2.0 * n_obs * devices, 9.0 * camera_slot.shape[0] + 3.0 * damping.shape[0] * devices)
     lines = lambda array: array.reshape(-1, LANES)
     res, cam, pt = row_major(residual), row_major(cam_jacobian), row_major(point_jacobian)
-    kept, rest, cost, norm = whole(
+    kept, rest, ends = whole(
         res, cam, pt, lines(obs_camera), lines(obs_slot), tile_offset, lines(damping), lines(camera_slot), sizes, scale
     )
-    return (kept + rest, cost.reshape(()), norm.reshape(()))
+    return (kept + rest, ends[0, 0], ends[0, 1])
 
 
 def solution(mesh):

time: 50.9 us -> 48.6 us (0.955)
  between operations: 4.14 us -> 0.64 us
  local copies, waits for them, and re-layouts: 0 us -> 1.33 us
    slice x0 -> x1, local copies, waits for them, and re-layouts: none -> 1.33 us  [on_device(): return (kept + rest, ends[0, 0], ends[0, 1])]
where the time goes in v7:
time: 48.6 us; the launch traced here: 48.3 us
  Pallas kernels  45 us (93%)
  local copies, waits for them, and re-layouts  1.33 us (3%)
  other arithmetic  1.32 us (3%)
  between operations  0.64 us (1%)
    pallas_call x1, Pallas kernels, whole(): pl.pallas_call(scoped(functools.partial(whole_kernel, sizes, scale), acc_...  45 us
    slice x1, local copies, waits for them, and re-layouts, on_device(): return (kept + rest, ends[0, 0], ends[0, 1])  1.33 us
    add x1, other arithmetic, on_device(): return (kept + rest, ends[0, 0], ends[0, 1])  1.32 us

profile of v7, /device:TPU:1, one launch (start us, length us, event | category | flops | bytes accessed | tf_op | source)
XLA Modules:
  0.0 48.3 jit_solution(14772961083655517667)
XLA Ops:
  0.6 45.0 %shard_map.103 = (f32[9,128]{1,0:T(8,128)}, f32[9,128]{1,0:T(8,128)}, f32[8,128]{1,0:T(8,128)}) custom-call(s32[32]{0:T(128)} %refs_0_.1, f32[256,128]{1,0:T(8,128)} %bitcast.23, f32[9,256,128]{2,1,0:T(8,128)} %bitcast.21, f32[3,256,128]{2,1,0:T(8,128)} %bitcast.22, s32[128,128]{1,0:T(8,128)} %bitcast.24, s32[128,128]{1,0:T(8,128)} %bitcast.25, ...), custom_call_target="tpu_custom_call" | custom-call | tf_op jit(solution)/shard_map/pallas_call | solution.py:553
  45.7 1.3 %add.3 = f32[9,128]{1,0:T(8,128)} add(f32[9,128]{1,0:T(8,128)} %get-tuple-element.6, f32[9,128]{1,0:T(8,128)} %get-tuple-element.7) | non-fusion elementwise | flops 1152 | bytes 13824 | tf_op jit(solution)/shard_map/add | solution.py:613
  47.0 1.3 %fusion = (f32[1,1]{1,0:T(1,128)}, f32[1,1]{1,0:T(1,128)}) fusion(f32[8,128]{1,0:T(8,128)} %get-tuple-element.8), kind=kLoop, calls=%fused_computation | loop fusion | bytes 16 | tf_op jit(solution)/shard_map/slice | solution.py:613

commit v8 on v7

--- a/solution.py
+++ b/solution.py
@@ -598,6 +598,26 @@
     )(tile_offset, residual, cam_jacobian, point_jacobian, obs_camera, obs_slot, damping, camera_slot)
 
 
+def close_kernel(kept_ref, rest_ref, ends_ref, reduced_ref, cost_ref, norm_ref):
+    reduced_ref[...] = kept_ref[...] + rest_ref[...]
+    lane = lax.broadcasted_iota(I32, (1, LANES), 1)
+    ends = ends_ref[0:1, :]
+    cost_ref[0, 0] = jnp.sum(jnp.where(lane == 0, ends, 0.0))
+    norm_ref[0, 0] = jnp.sum(jnp.where(lane == 1, ends, 0.0))
+
+
+def close(kept, rest, ends):
+    vmem = pl.BlockSpec(memory_space=pltpu.VMEM)
+    smem = pl.BlockSpec(memory_space=pltpu.SMEM)
+    scalar = jax.ShapeDtypeStruct((1, 1), F32)
+    return pl.pallas_call(
+        close_kernel,
+        out_shape=(jax.ShapeDtypeStruct(kept.shape, F32), scalar, scalar),
+        in_specs=[vmem] * 3,
+        out_specs=(vmem, smem, smem),
+    )(kept, rest, ends)
+
+
 def on_device(
     residual, cam_jacobian, point_jacobian, obs_camera, obs_slot, tile_offset, damping, camera_slot
 ):
@@ -610,7 +630,8 @@
     kept, rest, ends = whole(
         res, cam, pt, lines(obs_camera), lines(obs_slot), tile_offset, lines(damping), lines(camera_slot), sizes, scale
     )
-    return (kept + rest, ends[0, 0], ends[0, 1])
+    reduced, cost, norm = close(kept, rest, ends)
+    return (reduced, cost.reshape(()), norm.reshape(()))
 
 
 def solution(mesh):

time: 48.6 us -> 47.2 us (0.971)
  Pallas kernels: 45 us -> 46.4 us
  local copies, waits for them, and re-layouts: 1.33 us -> 0 us
  other arithmetic: 1.32 us -> 0 us
    pallas_call x0 -> x1, Pallas kernels: none -> 1.36 us  [close(): pl.pallas_call(close_kernel, out_shape=(jax.ShapeDtypeStruct(kept.shape,...]
    slice x1 -> x0, local copies, waits for them, and re-layouts: 1.33 us -> none  [on_device(): return (kept + rest, ends[0, 0], ends[0, 1])]
    add x1 -> x0, other arithmetic: 1.32 us -> none  [on_device(): return (kept + rest, ends[0, 0], ends[0, 1])]
where the time goes in v8:
time: 47.2 us; the launch traced here: 47 us
  Pallas kernels  46.4 us (98%)
  between operations  0.64 us (1%)
    pallas_call x1, Pallas kernels, whole(): pl.pallas_call(scoped(functools.partial(whole_kernel, sizes, scale), acc_...  45 us
    pallas_call x1, Pallas kernels, close(): pl.pallas_call(close_kernel, out_shape=(jax.ShapeDtypeStruct(kept.shape,...  1.36 us

profile of v8, /device:TPU:1, one launch (start us, length us, event | category | flops | bytes accessed | tf_op | source)
XLA Modules:
  0.0 47.0 jit_solution(2613833583415206566)
XLA Ops:
  0.6 45.0 %shard_map.103 = (f32[9,128]{1,0:T(8,128)}, f32[9,128]{1,0:T(8,128)}, f32[8,128]{1,0:T(8,128)}) custom-call(s32[32]{0:T(128)} %refs_0_.1, f32[256,128]{1,0:T(8,128)} %bitcast.23, f32[9,256,128]{2,1,0:T(8,128)} %bitcast.21, f32[3,256,128]{2,1,0:T(8,128)} %bitcast.22, s32[128,128]{1,0:T(8,128)} %bitcast.24, s32[128,128]{1,0:T(8,128)} %bitcast.25, ...), custom_call_target="tpu_custom_call" | custom-call | tf_op jit(solution)/shard_map/pallas_call | solution.py:553
  45.6 1.4 %shard_map.104 = (f32[9,128]{1,0:T(8,128)}, f32[1,1]{1,0:T(1,128)}, f32[1,1]{1,0:T(1,128)}) custom-call(f32[9,128]{1,0:T(8,128)} %get-tuple-element.9.kept_ref, f32[9,128]{1,0:T(8,128)} %get-tuple-element.10.rest_ref, f32[8,128]{1,0:T(8,128)} %get-tuple-element.11.ends_ref), custom_call_target="tpu_custom_call" | custom-call | tf_op jit(solution)/shard_map/pallas_call | solution.py:613

commit v9 on v8

--- a/solution.py
+++ b/solution.py
@@ -86,14 +86,15 @@
         total_ref[1, m * PITCH : m * PITCH + BINS] = total[:, LANES:]
 
 
-def regroup_into(out_ref, total_ref):
-    def one(hi, _):
+def regroup_slab(out_ref, total_ref, slab):
+    def one(k, _):
+        hi = slab * 16 + k
         for side in range(2):
             rows = pl.ds(hi, CAM, stride=PITCH)
-            out_ref[side, hi >> 4, (hi >> 2) & 3, hi & 3] = total_ref[side, rows, :]
+            out_ref[side, slab, k >> 2, k & 3] = total_ref[side, rows, :]
         return 0
 
-    lax.fori_loop(0, BINS, one, 0, unroll=4)
+    lax.fori_loop(0, 16, one, 0, unroll=4)
 
 
 def is_block(offset, count):
@@ -428,6 +429,7 @@
         flight[job] = []
         for k, dx in enumerate(SLABS):
             there = lax.rem(me["gx_0"] + dx, sizes["gx_0"])
+            regroup_slab(source, total_ref, there)
             flight[job].append(
                 send(
                     source.at[1 - core, there],
@@ -484,7 +486,6 @@
         loads,
     )
     drain(accs, total_ref)
-    regroup_into(grad_ref, total_ref)
     pl.semaphore_wait(barrier, len(far) + len(near) + len(others))
     pairs(0, grad_ref)
     point_square = solve_points(point_ref, damp_ref, step_ref)
@@ -518,7 +519,6 @@
     ]
     second_tiles(24, 32, *refs)
     drain(accs, total_ref)
-    regroup_into(move_ref, total_ref)
     pairs(1, move_ref)
     for copy in arrivals:
         copy.wait_recv()

time: 47.2 us -> 46.9 us (level)
  no operation moved by 1% of the time
where the time goes in v9:
time: 46.9 us; the launch traced here: 46.7 us
  Pallas kernels  46.1 us (98%)
  between operations  0.64 us (1%)
    pallas_call x1, Pallas kernels, whole(): pl.pallas_call(scoped(functools.partial(whole_kernel, sizes, scale), acc_...  44.7 us
    pallas_call x1, Pallas kernels, close(): pl.pallas_call(close_kernel, out_shape=(jax.ShapeDtypeStruct(kept.shape,...  1.36 us

profile of v9, /device:TPU:1, one launch (start us, length us, event | category | flops | bytes accessed | tf_op | source)
XLA Modules:
  0.0 46.7 jit_solution(15991915730277837660)
XLA Ops:
  0.6 44.7 %shard_map.103 = (f32[9,128]{1,0:T(8,128)}, f32[9,128]{1,0:T(8,128)}, f32[8,128]{1,0:T(8,128)}) custom-call(s32[32]{0:T(128)} %refs_0_.1, f32[256,128]{1,0:T(8,128)} %bitcast.23, f32[9,256,128]{2,1,0:T(8,128)} %bitcast.21, f32[3,256,128]{2,1,0:T(8,128)} %bitcast.22, s32[128,128]{1,0:T(8,128)} %bitcast.24, s32[128,128]{1,0:T(8,128)} %bitcast.25, ...), custom_call_target="tpu_custom_call" | custom-call | tf_op jit(solution)/shard_map/pallas_call | solution.py:553
  45.4 1.4 %shard_map.104 = (f32[9,128]{1,0:T(8,128)}, f32[1,1]{1,0:T(1,128)}, f32[1,1]{1,0:T(1,128)}) custom-call(f32[9,128]{1,0:T(8,128)} %get-tuple-element.9.kept_ref, f32[9,128]{1,0:T(8,128)} %get-tuple-element.10.rest_ref, f32[8,128]{1,0:T(8,128)} %get-tuple-element.11.ends_ref), custom_call_target="tpu_custom_call" | custom-call | tf_op jit(solution)/shard_map/pallas_call | solution.py:613

commit v10 on v8

--- a/solution.py
+++ b/solution.py
@@ -517,9 +517,6 @@
         for k, device in enumerate(far)
     ]
     second_tiles(24, 32, *refs)
-    drain(accs, total_ref)
-    regroup_into(move_ref, total_ref)
-    pairs(1, move_ref)
     for copy in arrivals:
         copy.wait_recv()
     plane_ref[...] = mine_ref[...] + jnp.sum(far_ref[...], axis=0)
@@ -527,6 +524,9 @@
         send(plane_ref, near_ref.at[k], near_send.at[k], near_recv.at[k], device)
         for k, device in enumerate(near)
     ]
+    drain(accs, total_ref)
+    regroup_into(move_ref, total_ref)
+    pairs(1, move_ref)
     spread(1, move_ref)
     for copy in arrivals:
         copy.wait_recv()

time: 47.2 us -> 48.1 us (1.019)
  Pallas kernels: 46.4 us -> 47.3 us
    pallas_call x1, Pallas kernels: 45 us -> 45.9 us  [whole(): pl.pallas_call(scoped(functools.partial(whole_kernel, sizes, scale), acc_...]
where the time goes in v10:
time: 48.1 us; the launch traced here: 47.9 us
  Pallas kernels  47.3 us (98%)
  between operations  0.64 us (1%)
    pallas_call x1, Pallas kernels, whole(): pl.pallas_call(scoped(functools.partial(whole_kernel, sizes, scale), acc_...  45.9 us
    pallas_call x1, Pallas kernels, close(): pl.pallas_call(close_kernel, out_shape=(jax.ShapeDtypeStruct(kept.shape,...  1.36 us

profile of v10, /device:TPU:1, one launch (start us, length us, event | category | flops | bytes accessed | tf_op | source)
XLA Modules:
  0.0 47.9 jit_solution(14295510543905260507)
XLA Ops:
  0.6 45.9 %shard_map.103 = (f32[9,128]{1,0:T(8,128)}, f32[9,128]{1,0:T(8,128)}, f32[8,128]{1,0:T(8,128)}) custom-call(s32[32]{0:T(128)} %refs_0_.1, f32[256,128]{1,0:T(8,128)} %bitcast.23, f32[9,256,128]{2,1,0:T(8,128)} %bitcast.21, f32[3,256,128]{2,1,0:T(8,128)} %bitcast.22, s32[128,128]{1,0:T(8,128)} %bitcast.24, s32[128,128]{1,0:T(8,128)} %bitcast.25, ...), custom_call_target="tpu_custom_call" | custom-call | tf_op jit(solution)/shard_map/pallas_call | solution.py:553
  46.6 1.4 %shard_map.104 = (f32[9,128]{1,0:T(8,128)}, f32[1,1]{1,0:T(1,128)}, f32[1,1]{1,0:T(1,128)}) custom-call(f32[9,128]{1,0:T(8,128)} %get-tuple-element.9.kept_ref, f32[9,128]{1,0:T(8,128)} %get-tuple-element.10.rest_ref, f32[8,128]{1,0:T(8,128)} %get-tuple-element.11.ends_ref), custom_call_target="tpu_custom_call" | custom-call | tf_op jit(solution)/shard_map/pallas_call | solution.py:613
